TPU v7x, 32 devices: a whole 2x2x4 slice. The times are simulated.
32 devices in a mesh: dp: 8 (over z, x), patch: 4 (over y, core).
Axes of the slice: x: 2, y: 2, z: 4, core: 2. Of those that a mesh axis runs over, the one named last changes fastest.
Arguments:
- query_rows: bfloat16 [8, 512, 576], P('dp', 'patch'), may hold values from -6 to 6
- key_rows: bfloat16 [8, 512, 576], P('dp', 'patch'), may hold values from -6 to 6
- value_rows: bfloat16 [8, 512, 576], P('dp', 'patch'), may hold values from -6 to 6
- out_weight: bfloat16 [576, 1152], replicated, may hold values from -0.25 to 0.25
- target: bfloat16 [8, 512, 1152], P('dp', 'patch'), may hold values from -6 to 6
- lengths: int32 [8], P('dp'), may hold values from 64 to 512
- segments: int32 [8, 512], P('dp', 'patch'), may hold values from 0 to 7, never falling along the last dimension, each value on 1 to 256 neighbouring positions
Outputs:
- query_grad: float32 [8, 512, 576], P('dp', 'patch')
- key_grad: float32 [8, 512, 576], P('dp', 'patch')
- value_grad: float32 [8, 512, 576], P('dp', 'patch')
- weight_grad: float32 [576, 1152], P('patch', 'dp')
- loss: float32 [], replicated
All inputs are finite; a program needn't handle non-finite values.
Results may differ from a plain program's by a relative error of at most 0.024.
Values may be sent and summed in bfloat16 or wider, within the bound.
A program may use at most 64 MiB of HBM per device.

v0:
```python
import functools
import math

import jax
import jax.numpy as jnp
from jax import lax
from jax.experimental import pallas as pl
from jax.experimental.pallas import tpu as pltpu
from jax.sharding import PartitionSpec as P

MESH = pl.DeviceIdType.MESH
WIDTH = 1152
HEADS = 8
HEAD_DIM = 72
FEAT = 576
PAIRS = HEADS // 2
PAIR_ROWS = 2 * HEAD_DIM
FEAT_PAD = 640
SPAN = 256
NEG_LARGE = -1e30
F32 = jnp.float32
BF16 = jnp.bfloat16
KEY, VALUE, QUERY, GRAD = range(4)


def nt(left, right):
    return lax.dot_general(left, right, (((1,), (1,)), ((), ())), preferred_element_type=F32)


def nn(left, right):
    return lax.dot_general(left, right, (((1,), (0,)), ((), ())), preferred_element_type=F32)


def tn(left, right):
    return lax.dot_general(left, right, (((0,), (0,)), ((), ())), preferred_element_type=F32)


def span_start(owner, features):
    return pl.multiple_of(jnp.minimum(owner * features // 128 * 128, FEAT_PAD - SPAN), 128)


def kernel(
    members,
    groups,
    len_ref,
    seg_ref,
    q_ref,
    k_ref,
    v_ref,
    w_hbm,
    t_hbm,
    dq_ref,
    dk_ref,
    dv_ref,
    dw_ref,
    sum_ref,
    w_ref,
    t_ref,
    seg_row_ref,
    all_ref,
    seg_own,
    seg_all,
    stat_own,
    stat_all,
    stat_columns,
    bias_ref,
    prob_ref,
    attn_ref,
    dout_ref,
    part_ref,
    w1_ref,
    keep_ref,
    wx_ref,
    w2_ref,
    wz_ref,
    w3_ref,
    fin_ref,
    w4_ref,
    tile_own,
    tile_all,
    sum_own,
    sum_all,
    load_sem,
    send_sem,
    recv_sem,
    seg_send,
    seg_recv,
    stat_send,
    stat_recv,
    tile_send,
    tile_recv,
    sum_send,
    sum_recv,
    s1,
    r1,
    s2,
    r2,
    s3,
    r3,
    s4,
    r4,
):
    rows = q_ref.shape[1]
    total = rows * members
    chips = members // 2
    half = groups // 2
    outer = groups // 2
    mine = outer // 2
    features = dw_ref.shape[0]
    me = lax.axis_index("patch")
    dp = lax.axis_index("dp")
    chip, core = me // 2, me % 2
    step_a, step_b = dp // 2, dp % 2
    partner = chip * 2 + 1 - core

    def patch_peer(shift):
        return lax.rem(me + shift, members)

    def dp_peer(shift):
        return lax.rem(dp + shift, groups)

    def far(shift):
        return lax.rem(chip + shift, chips)

    loads = [
        pltpu.make_async_copy(seg_ref, seg_row_ref, load_sem.at[0]),
        pltpu.make_async_copy(k_ref, all_ref.at[KEY, me], load_sem.at[1]),
        pltpu.make_async_copy(v_ref, all_ref.at[VALUE, me], load_sem.at[2]),
        pltpu.make_async_copy(q_ref, all_ref.at[QUERY, me], load_sem.at[3]),
        pltpu.make_async_copy(w_hbm, w_ref, load_sem.at[4]),
        pltpu.make_async_copy(t_hbm, t_ref, load_sem.at[5]),
    ]
    for load in loads:
        load.start()

    barrier = pltpu.get_barrier_semaphore()
    for shift in range(1, members):
        pl.semaphore_signal(barrier, inc=1, device_id=(dp, patch_peer(shift)), device_id_type=MESH)
    for shift in range(1, groups):
        pl.semaphore_signal(barrier, inc=1, device_id=(dp_peer(shift), me), device_id_type=MESH)
    loads[0].wait()
    seg_own[...] = jnp.broadcast_to(seg_row_ref[...], seg_own.shape)
    seg_all[me] = seg_own[...]
    for load in loads[1:4]:
        load.wait()
    pl.semaphore_wait(barrier, members + groups - 2)

    def copy(src, dst, send, recv, device):
        return pltpu.make_async_remote_copy(
            src_ref=src, dst_ref=dst, send_sem=send, recv_sem=recv, device_id=device, device_id_type=MESH
        )

    pending = []

    def start(item):
        item.start()
        pending.append(item)

    def rows_of(pair):
        return pl.ds(PAIR_ROWS * pair, PAIR_ROWS)

    def spread(array, pair):
        src = dst = all_ref.at[array, me, rows_of(pair)]
        recv = recv_sem.at[array, me, pair]
        for shift in range(1, chips):
            start(copy(src, dst, send_sem.at[array, shift, pair], recv, (dp, far(shift) * 2 + core)))
        start(copy(src, dst, send_sem.at[array, 0, pair], recv, (dp, partner)))

    def arrived(array, owner, pair):
        slot = all_ref.at[array, owner, rows_of(pair)]
        copy(slot, slot, send_sem.at[array, 0, pair], recv_sem.at[array, owner, pair], (dp, partner)).wait_recv()

    def relay(array, pair):
        for shift in range(1, chips):
            owner = far(shift) * 2 + core
            arrived(array, owner, pair)
            slot = all_ref.at[array, owner, rows_of(pair)]
            send = send_sem.at[array, chips - 1 + shift, pair]
            start(copy(slot, slot, send, recv_sem.at[array, owner, pair], (dp, partner)))

    def finish(array, pair):
        arrived(array, partner, pair)
        for shift in range(1, chips):
            arrived(array, far(shift) * 2 + 1 - core, pair)

    def small(own, everyone, send, recv):
        for shift in range(1, members):
            start(copy(own, everyone.at[me], send.at[shift], recv.at[me], (dp, patch_peer(shift))))

    def small_wait(own, everyone, send, recv):
        for shift in range(1, members):
            owner = patch_peer(shift)
            copy(own, everyone.at[owner], send.at[shift], recv.at[owner], (dp, owner)).wait_recv()

    small(seg_own, seg_all, seg_send, seg_recv)
    for pair in range(PAIRS):
        spread(KEY, pair)
        spread(VALUE, pair)
    for pair in range(PAIRS):
        spread(QUERY, pair)

    upper = lax.broadcasted_iota(jnp.int32, (PAIR_ROWS, 1), 0) < HEAD_DIM
    masks = [upper.astype(F32).astype(BF16), jnp.logical_not(upper).astype(F32).astype(BF16)]

    def stacked(value):
        return jnp.concatenate([value * masks[0], value * masks[1]], axis=1)

    def merged(value):
        return jnp.concatenate([value[:HEAD_DIM, :rows], value[HEAD_DIM:, rows:]], axis=0)

    def part_of(ref, pair):
        return ref[PAIR_ROWS * pair : PAIR_ROWS * (pair + 1), :]

    def own(array, pair):
        return all_ref[array, me, PAIR_ROWS * pair : PAIR_ROWS * (pair + 1), :]

    def whole(array, pair):
        low = PAIR_ROWS * pair
        return jnp.concatenate([all_ref[array, j, low : low + PAIR_ROWS, :] for j in range(members)], axis=1)

    length = len_ref[0]
    lane_position = lax.broadcasted_iota(jnp.int32, (1, rows), 1)
    own_live = me * rows + lax.broadcasted_iota(jnp.int32, (rows, 1), 0) < length
    own_group = jnp.where(me * rows + lane_position < length, seg_own[0:1], -1).astype(F32)
    small_wait(seg_own, seg_all, seg_send, seg_recv)
    for j in range(members):
        group = jnp.where(j * rows + lane_position < length, seg_all[j][0:1], -1).astype(F32)
        group = jnp.broadcast_to(group, (rows, rows)).T
        bias_ref[j * rows : (j + 1) * rows, :] = jnp.where(group == own_group, 0.0, NEG_LARGE)
    attn_ref[FEAT:, :] = jnp.zeros((FEAT_PAD - FEAT, rows), F32)

    log_scale = math.log2(math.e) / math.sqrt(HEAD_DIM)
    score_scale = 1.0 / math.sqrt(HEAD_DIM)

    def biased(scores):
        bias = bias_ref[...]
        return scores * log_scale + jnp.concatenate([bias, bias], axis=1)

    denoms = []
    for pair in range(PAIRS):
        relay(KEY, pair)
        relay(VALUE, pair)
        finish(KEY, pair)
        scores = biased(tn(whole(KEY, pair), stacked(own(QUERY, pair))))
        row_max = jnp.max(scores, axis=0, keepdims=True)
        probs = jnp.exp2(scores - row_max)
        denom = jnp.sum(probs, axis=0, keepdims=True)
        prob_ref[pair] = probs
        log_norm = row_max + jnp.log2(denom)
        for side in (0, 1):
            head = 2 * pair + side
            stat_own[head : head + 1, :] = log_norm[:, side * rows : (side + 1) * rows]
        denoms.append(denom)
        finish(VALUE, pair)
        accum = nn(whole(VALUE, pair), probs.astype(BF16))
        attn_ref[PAIR_ROWS * pair : PAIR_ROWS * (pair + 1), :] = merged(accum / denom)

    attn = attn_ref[...].T.astype(BF16)
    loads[4].wait()
    loads[5].wait()
    output = nn(attn[:, :FEAT], w_ref[...])
    error = jnp.where(own_live, output - t_ref[...].astype(F32), 0.0)
    dout_ref[...] = (2.0 * error).astype(BF16)

    share = WIDTH // groups
    part = tn(dout_ref[...], attn)
    for block in range(groups):
        part_ref[block] = part[block * share : (block + 1) * share].astype(BF16)
    first = core * half
    other = (1 - core) * half
    stage1 = copy(part_ref.at[pl.ds(other, half)], w1_ref, s1, r1, (dp, partner))
    start(stage1)

    for pair in range(PAIRS):
        grad = nt(part_of(w_ref, pair), dout_ref[...]).astype(BF16)
        all_ref[GRAD, me, PAIR_ROWS * pair : PAIR_ROWS * (pair + 1), :] = grad
        spread(GRAD, pair)
        attn_pair = part_of(attn_ref, pair).astype(BF16).astype(F32)
        product = grad.astype(F32) * attn_pair
        for side in (0, 1):
            head = HEADS + 2 * pair + side
            stat_own[head : head + 1, :] = jnp.sum(
                product[HEAD_DIM * side : HEAD_DIM * (side + 1)], axis=0, keepdims=True
            )
    small(stat_own, stat_all, stat_send, stat_recv)
    stat_all[me] = stat_own[...]
    loss_part = jnp.sum(jnp.sum(error * error, axis=0, keepdims=True), axis=1, keepdims=True)
    tile_own[...] = jnp.broadcast_to(loss_part, tile_own.shape)
    small(tile_own, tile_all, tile_send, tile_recv)

    def query_pass(pair):
        low = HEADS + 2 * pair
        delta = jnp.concatenate([stat_own[low : low + 1, :], stat_own[low + 1 : low + 2, :]], axis=1)
        dprobs = tn(whole(VALUE, pair), stacked(own(GRAD, pair)))
        dscores = prob_ref[pair] * (1.0 / denoms[pair]) * (dprobs - delta)
        value = nn(whole(KEY, pair), dscores.astype(BF16))
        dq_ref[PAIR_ROWS * pair : PAIR_ROWS * (pair + 1), :] = merged(value) * score_scale

    stage1.wait_recv()
    cut = -(-share // 32) * 16
    pieces = [(i, side) for i in range(mine) for side in (0, 1)]
    spans = [pl.ds(0, cut), pl.ds(cut, share - cut)]
    stage2 = {}
    for i, side in pieces:
        away, span = 2 * i + 1 - step_b, spans[side]
        wx_ref[i, span] = (part_ref[first + away, span].astype(F32) + w1_ref[away, span].astype(F32)).astype(BF16)
        item = copy(
            wx_ref.at[i, span],
            w2_ref.at[i, span],
            s2.at[i, side],
            r2.at[i, side],
            (step_a * 2 + 1 - step_b, me),
        )
        start(item)
        stage2[i, side] = item
    for i in range(mine):
        near = 2 * i + step_b
        keep_ref[i] = part_ref[first + near].astype(F32) + w1_ref[near].astype(F32)
    for pair in range(PAIRS):
        relay(QUERY, pair)

    query_pass(0)
    relay(GRAD, 0)
    relay(GRAD, 1)
    small_wait(stat_own, stat_all, stat_send, stat_recv)
    for j in range(members):
        tall = jnp.concatenate([stat_all[j], jnp.zeros((128 - 2 * HEADS, rows), F32)], axis=0)
        stat_columns[j * rows : (j + 1) * rows, :] = tall.T

    def third(i, side):
        span = spans[side]
        stage2[i, side].wait_recv()
        wz_ref[i, span] = (keep_ref[i, span] + w2_ref[i, span].astype(F32)).astype(BF16)
        owner = core * mine + i
        item = copy(
            wz_ref.at[i, span],
            w3_ref.at[step_a, span],
            s3.at[i, side],
            r3.at[step_a, side],
            (owner * 2 + step_b, me),
        )

        @pl.when(owner != step_a)
        def _():
            item.start()

        return owner, item

    def key_pass(pair):
        def columns(base):
            low = base + 2 * pair
            return jnp.concatenate(
                [jnp.broadcast_to(stat_columns[:, low + side : low + side + 1], (total, rows)) for side in (0, 1)],
                axis=1,
            )

        finish(QUERY, pair)
        finish(GRAD, pair)
        queries = whole(QUERY, pair)
        grads = whole(GRAD, pair)
        scores = biased(tn(queries, stacked(own(KEY, pair))))
        probs = jnp.exp2(scores - columns(0))
        dv_ref[PAIR_ROWS * pair : PAIR_ROWS * (pair + 1), :] = merged(nn(grads, probs.astype(BF16)))
        dprobs = tn(grads, stacked(own(VALUE, pair)))
        dscores = (probs * (dprobs - columns(HEADS))).astype(BF16)
        dk_ref[PAIR_ROWS * pair : PAIR_ROWS * (pair + 1), :] = merged(nn(queries, dscores)) * score_scale

    stage3 = [third(*pieces[0])]
    relay(GRAD, 2)
    relay(GRAD, 3)
    query_pass(1)
    stage3.append(third(*pieces[1]))
    query_pass(2)
    stage3.append(third(*pieces[2]))
    query_pass(3)
    stage3 += [third(*piece) for piece in pieces[3:]]

    small_wait(tile_own, tile_all, tile_send, tile_recv)
    tile_all[me] = tile_own[...]
    pack_loss = tile_all[0]
    for j in range(1, members):
        pack_loss = pack_loss + tile_all[j]
    tile_lane = lax.broadcasted_iota(jnp.int32, pack_loss.shape, 1)
    sum_own[...] = jnp.where(tile_lane == 0, pack_loss, length.astype(F32))
    for shift in range(1, groups):
        start(copy(sum_own, sum_all.at[dp], sum_send.at[shift], sum_recv.at[dp], (dp_peer(shift), me)))
    sum_all[dp] = sum_own[...]

    key_pass(0)
    key_pass(1)

    collect = step_a // mine
    is_collector = core == collect
    stage4 = []
    for shift in range(1, members):
        target = patch_peer(shift)
        span = fin_ref.at[:, pl.ds(span_start(target, features), SPAN)]
        stage4.append(copy(span, w4_ref.at[chip], s4.at[shift], r4.at[chip], (dp, target)))

    @pl.when(is_collector)
    def _():
        summed = wz_ref[step_a - core * mine].astype(F32)
        for shift in range(1, outer):
            source = lax.rem(step_a + shift, outer)
            for side, span in enumerate(spans):
                slot = w3_ref.at[source, span]
                copy(slot, slot, s3.at[0, side], r3.at[source, side], (source * 2 + step_b, me)).wait_recv()
            summed = summed + w3_ref[source].astype(F32)
        fin_ref[...] = summed.astype(BF16)
        for item in stage4:
            item.start()
        w4_ref[chip] = fin_ref[:, pl.ds(span_start(me, features), SPAN)]

    key_pass(2)
    key_pass(3)

    for shift in range(1, groups):
        source = dp_peer(shift)
        copy(sum_own, sum_all.at[source], sum_send.at[shift], sum_recv.at[source], (source, me)).wait_recv()
    totals = sum_all[0]
    for j in range(1, groups):
        totals = totals + sum_all[j]
    sum_ref[...] = totals

    def fetched(owner):
        copy(w4_ref.at[owner], w4_ref.at[owner], s4.at[0], r4.at[owner], (dp, partner)).wait_recv()

    @pl.when(jnp.logical_not(is_collector))
    def _():
        fetched(chip)

    for shift in range(1, chips):
        fetched(far(shift))
    shape = (features, SPAN)
    start_lane = me * features - span_start(me, features)
    chosen = (
        lax.broadcasted_iota(jnp.int32, shape, 1) == start_lane + lax.broadcasted_iota(jnp.int32, shape, 0)
    ).astype(F32).astype(BF16)
    result = nt(chosen, w4_ref[0])
    for j in range(1, chips):
        result = result + nt(chosen, w4_ref[j])
    dw_ref[...] = result

    for item in pending:
        item.wait_send()
    for owner, item in stage3:

        @pl.when(owner != step_a)
        def _():
            item.wait_send()

    @pl.when(is_collector)
    def _():
        for item in stage4:
            item.wait_send()


def scale_kernel(slots, total, sum_ref, dq_ref, dk_ref, dv_ref, dw_ref, query_ref, key_ref, value_ref, weight_ref, loss_ref):
    count = sum_ref[0:1, 1:2]
    ratio = slots / count
    query_ref[...] = dq_ref[...] * ratio
    key_ref[...] = dk_ref[...] * ratio
    value_ref[...] = dv_ref[...] * ratio
    weight_ref[...] = dw_ref[...] * (ratio / total)
    loss_ref[...] = sum_ref[0:1, 0:1] / (count * WIDTH)


def solution(mesh):
    members, groups = mesh.shape["patch"], mesh.shape["dp"]

    def local(query_rows, key_rows, value_rows, out_weight, target, lengths, segments):
        rows = query_rows.shape[1]
        total = rows * members
        chips = members // 2
        outer = groups // 2
        mine = outer // 2
        share = WIDTH // groups
        vmem = pl.BlockSpec(memory_space=pltpu.VMEM)
        hbm = pl.BlockSpec(memory_space=pltpu.HBM)
        dma = pltpu.SemaphoreType.DMA
        outs = pl.pallas_call(
            functools.partial(kernel, members, groups),
            out_shape=(
                jax.ShapeDtypeStruct((FEAT, rows), F32),
                jax.ShapeDtypeStruct((FEAT, rows), F32),
                jax.ShapeDtypeStruct((FEAT, rows), F32),
                jax.ShapeDtypeStruct((FEAT // members, share), F32),
                jax.ShapeDtypeStruct((8, 128), F32),
            ),
            in_specs=[pl.BlockSpec(memory_space=pltpu.SMEM)] + [hbm] * 6,
            out_specs=(vmem,) * 5,
            scratch_shapes=[
                pltpu.VMEM((FEAT, WIDTH), BF16),
                pltpu.VMEM((rows, WIDTH), BF16),
                pltpu.VMEM((1, rows), jnp.int32),
                pltpu.VMEM((4, members, FEAT, rows), BF16),
                pltpu.VMEM((8, rows), jnp.int32),
                pltpu.VMEM((members, 8, rows), jnp.int32),
                pltpu.VMEM((2 * HEADS, rows), F32),
                pltpu.VMEM((members, 2 * HEADS, rows), F32),
                pltpu.VMEM((total, 128), F32),
                pltpu.VMEM((total, rows), F32),
                pltpu.VMEM((PAIRS, total, 2 * rows), F32),
                pltpu.VMEM((FEAT_PAD, rows), F32),
                pltpu.VMEM((rows, WIDTH), BF16),
                pltpu.VMEM((groups, share, FEAT_PAD), BF16),
                pltpu.VMEM((groups // 2, share, FEAT_PAD), BF16),
                pltpu.VMEM((mine, share, FEAT_PAD), F32),
                pltpu.VMEM((mine, share, FEAT_PAD), BF16),
                pltpu.VMEM((mine, share, FEAT_PAD), BF16),
                pltpu.VMEM((mine, share, FEAT_PAD), BF16),
                pltpu.VMEM((outer, share, FEAT_PAD), BF16),
                pltpu.VMEM((share, FEAT_PAD), BF16),
                pltpu.VMEM((chips, share, SPAN), BF16),
                pltpu.VMEM((8, 128), F32),
                pltpu.VMEM((members, 8, 128), F32),
                pltpu.VMEM((8, 128), F32),
                pltpu.VMEM((groups, 8, 128), F32),
                dma((6,)),
                dma((4, members, PAIRS)),
                dma((4, members, PAIRS)),
                dma((members,)),
                dma((members,)),
                dma((members,)),
                dma((members,)),
                dma((members,)),
                dma((members,)),
                dma((groups,)),
                dma((groups,)),
                dma,
                dma,
                dma((mine, 2)),
                dma((mine, 2)),
                dma((mine, 2)),
                dma((outer, 2)),
                dma((members,)),
                dma((chips,)),
            ],
            compiler_params=pltpu.CompilerParams(collective_id=0, has_side_effects=True, vmem_limit_bytes=65900000),
            name="sublayer",
        )(
            lengths,
            segments,
            query_rows[0].T,
            key_rows[0].T,
            value_rows[0].T,
            out_weight,
            target[0],
        )
        final = pl.pallas_call(
            functools.partial(scale_kernel, groups * total, total),
            out_shape=(
                jax.ShapeDtypeStruct((FEAT, rows), F32),
                jax.ShapeDtypeStruct((FEAT, rows), F32),
                jax.ShapeDtypeStruct((FEAT, rows), F32),
                jax.ShapeDtypeStruct((FEAT // members, share), F32),
                jax.ShapeDtypeStruct((1, 1), F32),
            ),
            in_specs=[vmem] * 5,
            out_specs=(vmem,) * 5,
            compiler_params=pltpu.CompilerParams(vmem_limit_bytes=65900000),
            name="scale",
        )(outs[4], *outs[:4])
        return (final[0].T[None], final[1].T[None], final[2].T[None], final[3], final[4].reshape(()))

    placed = (
        P("dp", "patch", None),
        P("dp", "patch", None),
        P("dp", "patch", None),
        P(),
        P("dp", "patch", None),
        P("dp"),
        P("dp", "patch"),
    )
    return jax.shard_map(
        local,
        mesh=mesh,
        in_specs=placed,
        out_specs=(
            P("dp", "patch", None),
            P("dp", "patch", None),
            P("dp", "patch", None),
            P("patch", "dp"),
            P(),
        ),
        check_vma=False,
    )
```

profile of v0, /device:TPU:0, one launch (start us, length us, event | category | flops | bytes accessed | tf_op | source)
XLA Modules:
  0.0 42.6 jit_solution(2504933567489998463)
XLA Ops:
  1.3 39.0 %sublayer.1 = (f32[576,128]{1,0:T(8,128)}, f32[576,128]{1,0:T(8,128)}, f32[576,128]{1,0:T(8,128)}, f32[144,144]{1,0:T(8,128)}, f32[8,128]{1,0:T(8,128)}) custom-call(s32[1]{0:T(128)S(6)} %copy.12.len_ref, s32[1,128]{1,0:T(1,128)} %seg_ref.1, bf16[576,128]{1,0:T(8,128)(2,1)} %bitcast.21, bf16[576,128]{1,0:T(8,128)(2,1)} %bitcast.22, ...), custom_call_target="tpu_custom_call" | custom-call | tf_op jit(solution)/shard_map/sublayer/pallas_call | solution.py:481
  40.3 2.3 %scale.1 = (f32[576,128]{1,0:T(8,128)}, f32[576,128]{1,0:T(8,128)}, f32[576,128]{1,0:T(8,128)}, f32[144,144]{1,0:T(8,128)}, f32[1,1]{1,0:T(1,128)}) custom-call(f32[8,128]{1,0:T(8,128)} %get-tuple-element.15.sum_ref, f32[576,128]{1,0:T(8,128)} %get-tuple-element.16.dq_ref, f32[576,128]{1,0:T(8,128)} %get-tuple-element.17.dk_ref, ...), custom_call_target="tpu_custom_call" | custom-call | tf_op jit(solution)/shard_map/scale/pallas_call | solution.py:550
where the time goes:
time: 43.4 us; the launch traced here: 42.6 us
  Pallas kernels  41.3 us (95%)
  between operations  1.29 us (3%)
    pallas_call x1, Pallas kernels, local(): pl.pallas_call(functools.partial(kernel, members, groups), out_shape=(jax...  39 us
    pallas_call x1, Pallas kernels, local(): pl.pallas_call(functools.partial(scale_kernel, groups * total, total), ou...  2.27 us

commit v1 on v0

v1 whole, which is shorter than its diff:
```python
import functools
import math

import jax
import jax.numpy as jnp
from jax import lax
from jax.experimental import pallas as pl
from jax.experimental.pallas import tpu as pltpu
from jax.sharding import PartitionSpec as P

MESH = pl.DeviceIdType.MESH
WIDTH = 1152
HEADS = 8
HEAD_DIM = 72
FEAT = 576
PAIRS = HEADS // 2
PAIR_ROWS = 2 * HEAD_DIM
STAT_ROWS = 16
AUG_ROWS = PAIR_ROWS + STAT_ROWS
LANES = 128
NEG_LARGE = -1e30
F32 = jnp.float32
BF16 = jnp.bfloat16
KEY, VALUE, QUERY = range(3)


def nt(left, right):
    return lax.dot_general(left, right, (((1,), (1,)), ((), ())), preferred_element_type=F32)


def nn(left, right):
    return lax.dot_general(left, right, (((1,), (0,)), ((), ())), preferred_element_type=F32)


def tn(left, right):
    return lax.dot_general(left, right, (((0,), (0,)), ((), ())), preferred_element_type=F32)


def pad16(size):
    return -(-size // 16) * 16


def unit_layout(members, groups):
    share, features = WIDTH // groups, FEAT // members
    main = features // LANES * LANES
    rest = features - main
    main_rows = pad16(share) if main else 0
    tiles = -(-share // LANES)
    return share, features, main, rest, main_rows, tiles, main_rows + tiles * pad16(rest)


def kernel(
    members,
    groups,
    len_ref,
    seg_hbm,
    q_hbm,
    k_hbm,
    v_hbm,
    w_hbm,
    t_hbm,
    dq_ref,
    dk_ref,
    dv_ref,
    dw_ref,
    sum_ref,
    w_ref,
    t_ref,
    seg_row_ref,
    wt_ref,
    acc_ref,
    dout_ref,
    kvq_ref,
    g_ref,
    seg_own,
    seg_all,
    stat_ref,
    bias_ref,
    prob_ref,
    at_ref,
    dt_own,
    dt_all,
    u_own,
    y_all,
    z_own,
    z_all,
    tile_own,
    tile_all,
    sum_own,
    sum_all,
    load_sem,
    far_sem,
    near_sem,
    kvq_send,
    g_far,
    g_near,
    g_send,
    at_send,
    at_recv,
    dt_send,
    dt_recv,
    y_send,
    y_recv,
    z_send,
    z_recv,
    small_send,
    small_recv,
):
    rows = q_hbm.shape[1]
    chips = members // 2
    outer = groups // 2
    mine = outer // 2
    half = mine // 2
    share, features, main, rest, main_rows, tiles, unit_rows = unit_layout(members, groups)
    rest_rows = pad16(rest)
    me = lax.axis_index("patch")
    dp = lax.axis_index("dp")
    chip, core = me // 2, me % 2
    step_a, step_b = dp // 2, dp % 2
    partner = chip * 2 + 1 - core
    across = step_a * 2 + 1 - step_b
    slot = step_b * 2 + core

    def patch_peer(shift):
        return lax.rem(me + shift, members)

    def dp_peer(shift):
        return lax.rem(dp + shift, groups)

    def far(shift):
        return lax.rem(chip + shift, chips)

    def outer_peer(shift):
        return lax.rem(step_a + shift, outer)

    loads = [
        pltpu.make_async_copy(k_hbm, kvq_ref.at[KEY, me], load_sem.at[0]),
        pltpu.make_async_copy(v_hbm, kvq_ref.at[VALUE, me], load_sem.at[1]),
        pltpu.make_async_copy(seg_hbm, seg_row_ref, load_sem.at[2]),
        pltpu.make_async_copy(q_hbm, kvq_ref.at[QUERY, me], load_sem.at[3]),
        pltpu.make_async_copy(w_hbm, w_ref, load_sem.at[4]),
        pltpu.make_async_copy(t_hbm, t_ref, load_sem.at[5]),
    ]
    for load in loads:
        load.start()

    barrier = pltpu.get_barrier_semaphore()

    def greet(dp_index, patch_index):
        pl.semaphore_signal(barrier, inc=1, device_id=(dp_index, patch_index), device_id_type=MESH)

    for shift in range(1, members):
        greet(dp, patch_peer(shift))
    for shift in range(1, groups):
        greet(dp_peer(shift), me)
    greet(across, partner)
    for shift in range(1, outer):
        greet(outer_peer(shift) * 2 + step_b, partner)
    greeted = members - 1 + groups - 1 + 1 + outer - 1

    def copy(src, dst, send, recv, device):
        return pltpu.make_async_remote_copy(
            src_ref=src, dst_ref=dst, send_sem=send, recv_sem=recv, device_id=device, device_id_type=MESH
        )

    def received(ref, recv):
        copy(ref, ref, small_send.at[0], recv, (dp, partner)).wait_recv()

    def sent(ref, send):
        copy(ref, ref, send, small_recv.at[0], (dp, partner)).wait_send()

    def rows_of(pair):
        return pl.ds(PAIR_ROWS * pair, PAIR_ROWS)

    def kvq_part(array, owner, pair):
        if array == QUERY:
            return kvq_ref.at[array, owner]
        return kvq_ref.at[array, owner, rows_of(pair)]

    def kvq_index(array, pair):
        return 2 * PAIRS if array == QUERY else PAIRS * array + pair

    def spread(part, index, send, away, near):
        for shift in range(1, chips):
            copy(part, part, send, away.at[index], (dp, far(shift) * 2 + core)).start()
        copy(part, part, send, near.at[index], (dp, partner)).start()

    def relay_parts(part_at, span_at, index, send, away, near):
        received(part_at(far(1) * 2 + core) if chips == 2 else span_at(chips - 1), away.at[index])
        for shift in range(1, chips):
            part = part_at(far(shift) * 2 + core)
            copy(part, part, send, near.at[index], (dp, partner)).start()

    def kvq_span(array, pair, count):
        if array == QUERY:
            return kvq_ref.at[array, pl.ds(0, count)]
        return kvq_ref.at[array, pl.ds(0, count), rows_of(pair)]

    def kvq_spread(array, pair=0):
        spread(kvq_part(array, me, pair), kvq_index(array, pair), kvq_send.at[0], far_sem, near_sem)

    def kvq_relay(array, pair=0):
        relay_parts(
            lambda owner: kvq_part(array, owner, pair),
            lambda count: kvq_span(array, pair, count),
            kvq_index(array, pair),
            kvq_send.at[0],
            far_sem,
            near_sem,
        )

    def kvq_finish(array, pair=0):
        received(kvq_span(array, pair, chips), near_sem.at[kvq_index(array, pair)])

    def g_spread(pair):
        spread(g_ref.at[me, pair], pair, g_send.at[0], g_far, g_near)

    def g_relay(pair):
        relay_parts(
            lambda owner: g_ref.at[owner, pair],
            lambda count: g_ref.at[pl.ds(0, count), pair],
            pair,
            g_send.at[0],
            g_far,
            g_near,
        )

    def g_finish(pair):
        received(g_ref.at[pl.ds(0, chips), pair], g_near.at[pair])

    def small(index, own_ref, everyone):
        for shift in range(1, members):
            copy(own_ref, everyone.at[me], small_send.at[index], small_recv.at[index], (dp, patch_peer(shift))).start()

    loads[2].wait()
    seg_own[...] = jnp.broadcast_to(seg_row_ref[...], seg_own.shape)
    for load in (loads[0], loads[1], loads[3]):
        load.wait()
    pl.semaphore_wait(barrier, greeted)
    small(0, seg_own, seg_all)
    for pair in range(PAIRS):
        kvq_spread(KEY, pair)
        kvq_spread(VALUE, pair)
    kvq_spread(QUERY)
    seg_all[me] = seg_own[...]

    upper = lax.broadcasted_iota(jnp.int32, (PAIR_ROWS, 1), 0) < HEAD_DIM
    masks = [upper.astype(F32).astype(BF16), jnp.logical_not(upper).astype(F32).astype(BF16)]

    def stacked(value):
        return jnp.concatenate([value * masks[0], value * masks[1]], axis=1)

    def merged(value):
        return jnp.concatenate([value[:HEAD_DIM, :rows], value[HEAD_DIM:, rows:]], axis=0)

    def own(array, pair):
        return kvq_ref[array, me, PAIR_ROWS * pair : PAIR_ROWS * (pair + 1), :]

    def whole(array, pair):
        low = PAIR_ROWS * pair
        return jnp.concatenate([kvq_ref[array, j, low : low + PAIR_ROWS, :] for j in range(members)], axis=1)

    stat_row = lax.broadcasted_iota(jnp.int32, (STAT_ROWS, 2 * rows), 0)
    stat_side = (lax.broadcasted_iota(jnp.int32, (STAT_ROWS, 2 * rows), 1) >= rows).astype(jnp.int32)

    def picker(base):
        low = base + 3 * stat_side
        return jnp.where((stat_row >= low) & (stat_row < low + 3), -1.0, 0.0).astype(BF16)

    norm_picker, delta_picker = picker(0), picker(6)

    loads[5].wait()
    acc_ref[...] = -(t_ref[...].astype(F32).T)
    loads[4].wait()
    for pair in range(PAIRS):
        wt_ref[pair] = w_ref[PAIR_ROWS * pair : PAIR_ROWS * (pair + 1), :].astype(F32).T.astype(BF16)
    u_own[:, :, main_rows:, :] = jnp.zeros((mine, members, unit_rows - main_rows, LANES), BF16)

    length = len_ref[0]
    lane_position = lax.broadcasted_iota(jnp.int32, (1, rows), 1)
    own_live = me * rows + lane_position < length
    own_group = jnp.where(own_live, seg_own[0:1], -1).astype(F32)
    received(seg_all.at[pl.ds(0, members - 1)], small_recv.at[0])
    for j in range(members):
        group = jnp.where(j * rows + lane_position < length, seg_all[j][0:1], -1).astype(F32)
        group = jnp.broadcast_to(group, (rows, rows)).T
        bias_ref[j * rows : (j + 1) * rows, :] = jnp.where(group == own_group, 0.0, NEG_LARGE)

    log_scale = math.log2(math.e) / math.sqrt(HEAD_DIM)
    score_scale = 1.0 / math.sqrt(HEAD_DIM)

    def biased(scores):
        bias = bias_ref[...]
        return scores * log_scale + jnp.concatenate([bias, bias], axis=1)

    denoms = []
    kvq_relay(KEY, 0)
    for pair in range(PAIRS):
        kvq_finish(KEY, pair)
        kvq_relay(VALUE, pair)
        scores = biased(tn(whole(KEY, pair), stacked(own(QUERY, pair))))
        row_max = jnp.max(scores, axis=0, keepdims=True)
        probs = jnp.exp2(scores - row_max)
        denom = jnp.sum(probs, axis=0, keepdims=True)
        prob_ref[pair] = probs
        log_norm = (row_max + jnp.log2(denom)) * (1.0 / log_scale)
        for side in (0, 1):
            head = 2 * pair + side
            stat_ref[head : head + 1, :] = log_norm[:, side * rows : (side + 1) * rows]
        denoms.append(denom)
        if pair + 1 < PAIRS:
            kvq_relay(KEY, pair + 1)
        kvq_finish(VALUE, pair)
        accum = nn(whole(VALUE, pair), probs.astype(BF16))
        attn_pair = merged(accum / denom).astype(BF16)
        at_ref[slot, PAIR_ROWS * pair : PAIR_ROWS * (pair + 1), :] = attn_pair
        part = at_ref.at[slot, rows_of(pair)]
        copy(part, part, at_send.at[0], at_recv.at[0], (across, me)).start()
        copy(part, part, at_send.at[0], at_recv.at[1], (dp, partner)).start()
        acc_ref[...] += nn(wt_ref[pair], attn_pair)

    error = jnp.where(own_live, acc_ref[...], 0.0)
    dout = (2.0 * error).astype(BF16)
    dout_ref[...] = dout
    for z in range(outer):
        for side in (0, 1):
            low = (z * 2 + side) * share
            dt_own[side, z] = dout[low : low + share]
    for chunk in (0, 1):
        for side, to in ((1 - step_b, core), (1 - step_b, 1 - core), (step_b, 1 - core)):
            copy(
                dt_own.at[side, pl.ds(to * mine + chunk * half, half)],
                dt_all.at[pl.ds(chunk * half, half), slot],
                dt_send.at[0],
                dt_recv.at[chunk],
                (step_a * 2 + side, chip * 2 + to),
            ).start()
    for i in range(mine):
        dt_all[i, slot] = dt_own[step_b, core * mine + i]

    def terms(value):
        first = value.astype(BF16).astype(F32)
        second = (value - first).astype(BF16).astype(F32)
        return [first, second, value - first - second]

    for pair in range(PAIRS):
        grad = nn(w_ref[PAIR_ROWS * pair : PAIR_ROWS * (pair + 1), :], dout_ref[...]).astype(BF16)
        g_ref[me, pair, :PAIR_ROWS, :] = grad
        product = grad.astype(F32) * at_ref[slot, PAIR_ROWS * pair : PAIR_ROWS * (pair + 1), :].astype(F32)
        lines = []
        for side in (0, 1):
            lines += terms(stat_ref[2 * pair + side : 2 * pair + side + 1, :])
        for side in (0, 1):
            head = 2 * pair + side
            delta = jnp.sum(product[HEAD_DIM * side : HEAD_DIM * (side + 1)], axis=0, keepdims=True)
            stat_ref[HEADS + head : HEADS + head + 1, :] = delta
            lines += terms(delta)
        lines.append(jnp.zeros((STAT_ROWS - 12, rows), F32))
        g_ref[me, pair, PAIR_ROWS:, :] = jnp.concatenate(lines, axis=0).astype(BF16)
        g_spread(pair)

    loss_part = jnp.sum(jnp.sum(error * error, axis=0, keepdims=True), axis=1, keepdims=True)
    tile_own[...] = jnp.broadcast_to(loss_part, tile_own.shape)
    small(1, tile_own, tile_all)
    tile_all[me] = tile_own[...]

    def query_pass(pair):
        low = HEADS + 2 * pair
        delta = jnp.concatenate([stat_ref[low : low + 1, :], stat_ref[low + 1 : low + 2, :]], axis=1)
        grad = g_ref[me, pair, :PAIR_ROWS, :]
        dprobs = tn(whole(VALUE, pair), stacked(grad))
        dscores = prob_ref[pair] * (1.0 / denoms[pair]) * (dprobs - delta)
        value = nn(whole(KEY, pair), dscores.astype(BF16))
        dq_ref[PAIR_ROWS * pair : PAIR_ROWS * (pair + 1), :] = merged(value) * score_scale

    def key_pass(pair):
        g_finish(pair)
        queries = whole(QUERY, pair)
        grads = jnp.concatenate([g_ref[j, pair] for j in range(members)], axis=1)
        stats = grads[PAIR_ROWS:]
        scores = tn(
            jnp.concatenate([queries, stats], axis=0),
            jnp.concatenate([stacked(own(KEY, pair)), norm_picker], axis=0),
        )
        probs = jnp.exp2(biased(scores))
        dv_ref[PAIR_ROWS * pair : PAIR_ROWS * (pair + 1), :] = merged(nn(grads[:PAIR_ROWS], probs.astype(BF16)))
        dprobs = tn(grads, jnp.concatenate([stacked(own(VALUE, pair)), delta_picker], axis=0))
        dscores = (probs * dprobs).astype(BF16)
        dk_ref[PAIR_ROWS * pair : PAIR_ROWS * (pair + 1), :] = merged(nn(queries, dscores)) * score_scale

    def weight_part(chunk):
        received(dt_all.at[pl.ds(chunk * half, half), pl.ds(0, 3)], dt_recv.at[chunk])
        attn = jnp.concatenate([at_ref[s] for s in range(4)], axis=1)
        if main:
            attn_main = jnp.concatenate([attn[p * features : p * features + main] for p in range(members)], axis=0)
            attn_rest = jnp.concatenate([attn[p * features + main : (p + 1) * features] for p in range(members)], axis=0)
        else:
            attn_rest = attn
        for i in range(chunk * half, (chunk + 1) * half):
            grads = jnp.concatenate([dt_all[i, s] for s in range(4)], axis=1)
            if main:
                part_main = nt(grads, attn_main).astype(BF16)
            part_rest = nt(attn_rest, grads)
            for p in range(members):
                if main:
                    u_own[i, p, :share, :] = part_main[:, p * main : (p + 1) * main]
                for t in range(tiles):
                    wide = min(share - t * LANES, LANES)
                    piece = part_rest[p * rest : (p + 1) * rest, t * LANES : t * LANES + wide].astype(BF16)
                    low = main_rows + t * rest_rows
                    u_own[i, p, low : low + rest, :wide] = piece
            for to in (0, 1):
                for shift in range(1, chips):
                    copy(
                        u_own.at[i, far(shift) * 2 + to],
                        y_all.at[i, to, chip],
                        y_send.at[0],
                        y_recv.at[i, to],
                        (dp, far(shift) * 2 + core),
                    ).start()

    def weight_sum(i, to):
        received(y_all.at[i, to, pl.ds(0, chips - 1)], y_recv.at[i, to])
        value = u_own[i, chip * 2 + to].astype(F32)
        for shift in range(1, chips):
            value = value + y_all[i, to, far(shift)].astype(F32)
        z_own[i, to] = value.astype(BF16)
        target = core * mine + i
        stays = jnp.logical_and(target == step_a, core == to)

        @pl.when(stays)
        def _():
            z_all[step_a] = z_own[i, to]

        @pl.when(jnp.logical_not(stays))
        def _():
            copy(
                z_own.at[i, to],
                z_all.at[step_a],
                z_send.at[0],
                z_recv.at[0],
                (target * 2 + step_b, chip * 2 + to),
            ).start()

    kvq_relay(QUERY)
    received(at_ref.at[0], at_recv.at[0])
    part = at_ref.at[(1 - step_b) * 2 + core]
    copy(part, part, at_send.at[0], at_recv.at[1], (dp, partner)).start()
    query_pass(0)
    g_relay(0)
    query_pass(1)
    g_relay(1)
    received(at_ref.at[pl.ds(0, 2)], at_recv.at[1])
    weight_part(0)
    g_relay(2)
    query_pass(2)
    weight_part(1)
    g_relay(3)

    received(tile_all.at[pl.ds(0, members - 1)], small_recv.at[1])
    pack_loss = tile_all[0]
    for j in range(1, members):
        pack_loss = pack_loss + tile_all[j]
    tile_lane = lax.broadcasted_iota(jnp.int32, pack_loss.shape, 1)
    sum_own[...] = jnp.where(tile_lane == 0, pack_loss, length.astype(F32))
    for shift in range(1, groups):
        copy(sum_own, sum_all.at[dp], small_send.at[2], small_recv.at[2], (dp_peer(shift), me)).start()
    sum_all[dp] = sum_own[...]

    query_pass(3)
    kvq_finish(QUERY)
    key_pass(0)
    units = [(i, to) for i in range(mine) for to in (0, 1)]
    quarter = len(units) // 4
    for i, to in units[: 2 * quarter]:
        weight_sum(i, to)
    key_pass(1)
    for i, to in units[2 * quarter : 3 * quarter]:
        weight_sum(i, to)
    key_pass(2)
    for i, to in units[3 * quarter :]:
        weight_sum(i, to)
    key_pass(3)

    received(sum_all.at[pl.ds(0, groups - 1)], small_recv.at[2])
    totals = sum_all[0]
    for j in range(1, groups):
        totals = totals + sum_all[j]
    sum_ref[...] = totals

    sent(kvq_ref.at[:, pl.ds(0, members - 1)], kvq_send.at[0])
    sent(g_ref.at[pl.ds(0, members - 1)], g_send.at[0])
    sent(at_ref.at[pl.ds(0, 3)], at_send.at[0])
    sent(dt_all.at[:, pl.ds(0, 3)], dt_send.at[0])
    sent(y_all.at[:, :, pl.ds(0, chips - 1)], y_send.at[0])
    sent(seg_all.at[pl.ds(0, members - 1)], small_send.at[0])
    sent(tile_all.at[pl.ds(0, members - 1)], small_send.at[1])
    sent(sum_all.at[pl.ds(0, groups - 1)], small_send.at[2])

    collects = core == step_a // mine

    @pl.when(collects)
    def _():
        sent(z_all.at[pl.ds(0, outer - 1)], z_send.at[0])
        received(z_all.at[pl.ds(0, outer - 1)], z_recv.at[0])

    @pl.when(jnp.logical_not(collects))
    def _():
        sent(z_all, z_send.at[0])
        received(z_all, z_recv.at[0])

    summed = z_all[0].astype(F32)
    for j in range(1, outer):
        summed = summed + z_all[j].astype(F32)
    if main:
        dw_ref[:main, :] = summed[:share].T
    for t in range(tiles):
        wide = min(share - t * LANES, LANES)
        low = main_rows + t * rest_rows
        dw_ref[main:, t * LANES : t * LANES + wide] = summed[low : low + rest, :wide]


def scale_kernel(slots, total, sum_ref, dq_ref, dk_ref, dv_ref, dw_ref, query_ref, key_ref, value_ref, weight_ref, loss_ref):
    count = sum_ref[0:1, 1:2]
    ratio = slots / count
    query_ref[...] = dq_ref[...] * ratio
    key_ref[...] = dk_ref[...] * ratio
    value_ref[...] = dv_ref[...] * ratio
    weight_ref[...] = dw_ref[...] * (ratio / total)
    loss_ref[...] = sum_ref[0:1, 0:1] / (count * WIDTH)


def solution(mesh):
    members, groups = mesh.shape["patch"], mesh.shape["dp"]

    def local(query_rows, key_rows, value_rows, out_weight, target, lengths, segments):
        rows = query_rows.shape[1]
        total = rows * members
        chips = members // 2
        outer = groups // 2
        mine = outer // 2
        share, features, main, rest, main_rows, tiles, unit_rows = unit_layout(members, groups)
        vmem = pl.BlockSpec(memory_space=pltpu.VMEM)
        hbm = pl.BlockSpec(memory_space=pltpu.HBM)
        dma = pltpu.SemaphoreType.DMA
        operands = (
            segments,
            query_rows[0].T,
            key_rows[0].T,
            value_rows[0].T,
            out_weight,
            target[0],
        )
        outs = pl.pallas_call(
            functools.partial(kernel, members, groups),
            out_shape=(
                jax.ShapeDtypeStruct((FEAT, rows), F32),
                jax.ShapeDtypeStruct((FEAT, rows), F32),
                jax.ShapeDtypeStruct((FEAT, rows), F32),
                jax.ShapeDtypeStruct((features, share), F32),
                jax.ShapeDtypeStruct((8, 128), F32),
            ),
            in_specs=[pl.BlockSpec(memory_space=pltpu.SMEM)] + [hbm] * 6,
            out_specs=(vmem,) * 5,
            scratch_shapes=[
                pltpu.VMEM((FEAT, WIDTH), BF16),
                pltpu.VMEM((rows, WIDTH), BF16),
                pltpu.VMEM((1, rows), jnp.int32),
                pltpu.VMEM((PAIRS, WIDTH, PAIR_ROWS), BF16),
                pltpu.VMEM((WIDTH, rows), F32),
                pltpu.VMEM((WIDTH, rows), BF16),
                pltpu.VMEM((3, members, FEAT, rows), BF16),
                pltpu.VMEM((members, PAIRS, AUG_ROWS, rows), BF16),
                pltpu.VMEM((8, rows), jnp.int32),
                pltpu.VMEM((members, 8, rows), jnp.int32),
                pltpu.VMEM((2 * HEADS, rows), F32),
                pltpu.VMEM((total, rows), F32),
                pltpu.VMEM((PAIRS, total, 2 * rows), F32),
                pltpu.VMEM((4, FEAT, rows), BF16),
                pltpu.VMEM((2, outer, share, rows), BF16),
                pltpu.VMEM((mine, 4, share, rows), BF16),
                pltpu.VMEM((mine, members, unit_rows, LANES), BF16),
                pltpu.VMEM((mine, 2, chips, unit_rows, LANES), BF16),
                pltpu.VMEM((mine, 2, unit_rows, LANES), BF16),
                pltpu.VMEM((outer, unit_rows, LANES), BF16),
                pltpu.VMEM((8, 128), F32),
                pltpu.VMEM((members, 8, 128), F32),
                pltpu.VMEM((8, 128), F32),
                pltpu.VMEM((groups, 8, 128), F32),
                dma((6,)),
                dma((2 * PAIRS + 1,)),
                dma((2 * PAIRS + 1,)),
                dma((1,)),
                dma((PAIRS,)),
                dma((PAIRS,)),
                dma((1,)),
                dma((1,)),
                dma((2,)),
                dma((1,)),
                dma((2,)),
                dma((1,)),
                dma((mine, 2)),
                dma((1,)),
                dma((1,)),
                dma((3,)),
                dma((3,)),
            ],
            compiler_params=pltpu.CompilerParams(collective_id=0, has_side_effects=True, vmem_limit_bytes=48000000),
            name="sublayer",
        )(lengths, *[pltpu.with_memory_space_constraint(operand, pltpu.HBM) for operand in operands])
        final = pl.pallas_call(
            functools.partial(scale_kernel, groups * total, total),
            out_shape=(
                jax.ShapeDtypeStruct((FEAT, rows), F32),
                jax.ShapeDtypeStruct((FEAT, rows), F32),
                jax.ShapeDtypeStruct((FEAT, rows), F32),
                jax.ShapeDtypeStruct((features, share), F32),
                jax.ShapeDtypeStruct((1, 1), F32),
            ),
            in_specs=[vmem] * 5,
            out_specs=(vmem,) * 5,
            compiler_params=pltpu.CompilerParams(vmem_limit_bytes=8000000),
            name="scale",
        )(outs[4], *outs[:4])
        return (final[0].T[None], final[1].T[None], final[2].T[None], final[3], final[4].reshape(()))

    placed = (
        P("dp", "patch", None),
        P("dp", "patch", None),
        P("dp", "patch", None),
        P(),
        P("dp", "patch", None),
        P("dp"),
        P("dp", "patch"),
    )
    return jax.shard_map(
        local,
        mesh=mesh,
        in_specs=placed,
        out_specs=(
            P("dp", "patch", None),
            P("dp", "patch", None),
            P("dp", "patch", None),
            P("patch", "dp"),
            P(),
        ),
        check_vma=False,
    )
```

time: 43.4 us -> 33.5 us (0.77); the launches traced: 42.6 us -> 33.3 us
  Pallas kernels: 41.3 us -> 32 us
    pallas_call x1, Pallas kernels: 39 us -> 30.9 us  [local(): pl.pallas_call(functools.partial(kernel, members, groups), out_shape=(jax...]
    pallas_call x1, Pallas kernels: 2.27 us -> 1.09 us  [local(): pl.pallas_call(functools.partial(scale_kernel, groups * total, total), ou...]
where the time goes in v1:
time: 33.5 us; the launch traced here: 33.3 us
  Pallas kernels  32 us (96%)
  between operations  1.29 us (4%)
    pallas_call x1, Pallas kernels, local(): pl.pallas_call(functools.partial(kernel, members, groups), out_shape=(jax...  30.9 us
    pallas_call x1, Pallas kernels, local(): pl.pallas_call(functools.partial(scale_kernel, groups * total, total), ou...  1.09 us

profile of v1, /device:TPU:0, one launch (start us, length us, event | category | flops | bytes accessed | tf_op | source)
XLA Modules:
  0.0 33.3 jit_solution(4167314499535250473)
XLA Ops:
  1.3 30.9 %sublayer.1 = (f32[576,128]{1,0:T(8,128)S(1)}, f32[576,128]{1,0:T(8,128)S(1)}, f32[576,128]{1,0:T(8,128)S(1)}, f32[144,144]{1,0:T(8,128)S(1)}, f32[8,128]{1,0:T(8,128)S(1)}) custom-call(s32[1]{0:T(128)S(6)} %copy.12.len_ref, s32[1,128]{1,0:T(1,128)} %seg_hbm.1, bf16[576,128]{1,0:T(8,128)(2,1)} %bitcast.21, bf16[576,128]{1,0:T(8,128)(2,1)} %bitcast.22, ...), custom_call_target="tpu_custom_call" | custom-call | tf_op jit(solution)/shard_map/sublayer/pallas_call | solution.py:554
  32.2 1.1 %scale.1 = (f32[576,128]{1,0:T(8,128)}, f32[576,128]{1,0:T(8,128)}, f32[576,128]{1,0:T(8,128)}, f32[144,144]{1,0:T(8,128)}, f32[1,1]{1,0:T(1,128)}) custom-call(f32[8,128]{1,0:T(8,128)S(1)} %get-tuple-element.15.sum_ref, f32[576,128]{1,0:T(8,128)S(1)} %get-tuple-element.16.dq_ref, f32[576,128]{1,0:T(8,128)S(1)} %get-tuple-element.17.dk_ref, ...), custom_call_target="tpu_custom_call" | custom-call | tf_op jit(solution)/shard_map/scale/pallas_call | solution.py:611

commit v2 on v1

--- a/solution.py
+++ b/solution.py
@@ -66,7 +66,6 @@
     sum_ref,
     w_ref,
     t_ref,
-    seg_row_ref,
     wt_ref,
     acc_ref,
     dout_ref,
@@ -86,6 +85,8 @@
     z_all,
     tile_own,
     tile_all,
+    pair_own,
+    pair_all,
     sum_own,
     sum_all,
     load_sem,
@@ -105,6 +106,7 @@
     z_recv,
     small_send,
     small_recv,
+    wave_sem,
 ):
     rows = q_hbm.shape[1]
     chips = members // 2
@@ -124,9 +126,6 @@
     def patch_peer(shift):
         return lax.rem(me + shift, members)
 
-    def dp_peer(shift):
-        return lax.rem(dp + shift, groups)
-
     def far(shift):
         return lax.rem(chip + shift, chips)
 
@@ -136,7 +135,7 @@
     loads = [
         pltpu.make_async_copy(k_hbm, kvq_ref.at[KEY, me], load_sem.at[0]),
         pltpu.make_async_copy(v_hbm, kvq_ref.at[VALUE, me], load_sem.at[1]),
-        pltpu.make_async_copy(seg_hbm, seg_row_ref, load_sem.at[2]),
+        pltpu.make_async_copy(seg_hbm, seg_own, load_sem.at[2]),
         pltpu.make_async_copy(q_hbm, kvq_ref.at[QUERY, me], load_sem.at[3]),
         pltpu.make_async_copy(w_hbm, w_ref, load_sem.at[4]),
         pltpu.make_async_copy(t_hbm, t_ref, load_sem.at[5]),
@@ -151,12 +150,40 @@
 
     for shift in range(1, members):
         greet(dp, patch_peer(shift))
-    for shift in range(1, groups):
-        greet(dp_peer(shift), me)
-    greet(across, partner)
-    for shift in range(1, outer):
-        greet(outer_peer(shift) * 2 + step_b, partner)
-    greeted = members - 1 + groups - 1 + 1 + outer - 1
+    for to in (me, partner):
+        greet(across, to)
+
+        @pl.when(step_a > 0)
+        def _():
+            greet(dp - 2, to)
+
+        @pl.when(step_a < outer - 1)
+        def _():
+            greet(dp + 2, to)
+
+    edges = (step_a == 0).astype(jnp.int32) + (step_a == outer - 1).astype(jnp.int32)
+    greeted = members - 1 + 2 + 2 * (2 - edges)
+
+    def token(device, side):
+        pl.semaphore_signal(wave_sem.at[side], inc=1, device_id=(device, me), device_id_type=MESH)
+
+    def wave_start():
+        @pl.when(step_a > 0)
+        def _():
+            token(dp - 2, 1)
+
+        @pl.when(step_a < outer - 1)
+        def _():
+            token(dp + 2, 0)
+
+    def wave_wait():
+        @pl.when(step_a > 0)
+        def _():
+            pl.semaphore_wait(wave_sem.at[0], 1)
+
+        @pl.when(step_a < outer - 1)
+        def _():
+            pl.semaphore_wait(wave_sem.at[1], 1)
 
     def copy(src, dst, send, recv, device):
         return pltpu.make_async_remote_copy(
@@ -232,9 +259,7 @@
         for shift in range(1, members):
             copy(own_ref, everyone.at[me], small_send.at[index], small_recv.at[index], (dp, patch_peer(shift))).start()
 
-    loads[2].wait()
-    seg_own[...] = jnp.broadcast_to(seg_row_ref[...], seg_own.shape)
-    for load in (loads[0], loads[1], loads[3]):
+    for load in (loads[2], loads[0], loads[1], loads[3]):
         load.wait()
     pl.semaphore_wait(barrier, greeted)
     small(0, seg_own, seg_all)
@@ -242,6 +267,7 @@
         kvq_spread(KEY, pair)
         kvq_spread(VALUE, pair)
     kvq_spread(QUERY)
+    wave_start()
     seg_all[me] = seg_own[...]
 
     upper = lax.broadcasted_iota(jnp.int32, (PAIR_ROWS, 1), 0) < HEAD_DIM
@@ -279,10 +305,10 @@
     length = len_ref[0]
     lane_position = lax.broadcasted_iota(jnp.int32, (1, rows), 1)
     own_live = me * rows + lane_position < length
-    own_group = jnp.where(own_live, seg_own[0:1], -1).astype(F32)
+    own_group = jnp.where(own_live, seg_own[...], -1).astype(F32)
     received(seg_all.at[pl.ds(0, members - 1)], small_recv.at[0])
     for j in range(members):
-        group = jnp.where(j * rows + lane_position < length, seg_all[j][0:1], -1).astype(F32)
+        group = jnp.where(j * rows + lane_position < length, seg_all[j], -1).astype(F32)
         group = jnp.broadcast_to(group, (rows, rows)).T
         bias_ref[j * rows : (j + 1) * rows, :] = jnp.where(group == own_group, 0.0, NEG_LARGE)
 
@@ -318,6 +344,10 @@
         copy(part, part, at_send.at[0], at_recv.at[0], (across, me)).start()
         copy(part, part, at_send.at[0], at_recv.at[1], (dp, partner)).start()
         acc_ref[...] += nn(wt_ref[pair], attn_pair)
+        if pair == 2 and outer > 2:
+            wave_wait()
+            if outer > 3:
+                wave_start()
 
     error = jnp.where(own_live, acc_ref[...], 0.0)
     dout = (2.0 * error).astype(BF16)
@@ -442,6 +472,10 @@
                 (target * 2 + step_b, chip * 2 + to),
             ).start()
 
+    for hops in range(4, outer + 1):
+        wave_wait()
+        if hops < outer:
+            wave_start()
     kvq_relay(QUERY)
     received(at_ref.at[0], at_recv.at[0])
     part = at_ref.at[(1 - step_b) * 2 + core]
@@ -462,10 +496,8 @@
     for j in range(1, members):
         pack_loss = pack_loss + tile_all[j]
     tile_lane = lax.broadcasted_iota(jnp.int32, pack_loss.shape, 1)
-    sum_own[...] = jnp.where(tile_lane == 0, pack_loss, length.astype(F32))
-    for shift in range(1, groups):
-        copy(sum_own, sum_all.at[dp], small_send.at[2], small_recv.at[2], (dp_peer(shift), me)).start()
-    sum_all[dp] = sum_own[...]
+    pair_own[...] = jnp.where(tile_lane == 0, pack_loss, length.astype(F32))
+    copy(pair_own, pair_all, small_send.at[3], small_recv.at[3], (across, me)).start()
 
     query_pass(3)
     kvq_finish(QUERY)
@@ -474,6 +506,12 @@
     quarter = len(units) // 4
     for i, to in units[: 2 * quarter]:
         weight_sum(i, to)
+    received(pair_all, small_recv.at[3])
+    sum_own[...] = pair_own[...] + pair_all[...]
+    for shift in range(1, outer):
+        to = outer_peer(shift) * 2 + step_b
+        copy(sum_own, sum_all.at[step_a], small_send.at[2], small_recv.at[2], (to, me)).start()
+    sum_all[step_a] = sum_own[...]
     key_pass(1)
     for i, to in units[2 * quarter : 3 * quarter]:
         weight_sum(i, to)
@@ -482,9 +520,9 @@
         weight_sum(i, to)
     key_pass(3)
 
-    received(sum_all.at[pl.ds(0, groups - 1)], small_recv.at[2])
+    received(sum_all.at[pl.ds(0, outer - 1)], small_recv.at[2])
     totals = sum_all[0]
-    for j in range(1, groups):
+    for j in range(1, outer):
         totals = totals + sum_all[j]
     sum_ref[...] = totals
 
@@ -495,7 +533,8 @@
     sent(y_all.at[:, :, pl.ds(0, chips - 1)], y_send.at[0])
     sent(seg_all.at[pl.ds(0, members - 1)], small_send.at[0])
     sent(tile_all.at[pl.ds(0, members - 1)], small_send.at[1])
-    sent(sum_all.at[pl.ds(0, groups - 1)], small_send.at[2])
+    sent(sum_all.at[pl.ds(0, outer - 1)], small_send.at[2])
+    sent(pair_all, small_send.at[3])
 
     collects = core == step_a // mine
 
@@ -565,14 +604,13 @@
             scratch_shapes=[
                 pltpu.VMEM((FEAT, WIDTH), BF16),
                 pltpu.VMEM((rows, WIDTH), BF16),
-                pltpu.VMEM((1, rows), jnp.int32),
                 pltpu.VMEM((PAIRS, WIDTH, PAIR_ROWS), BF16),
                 pltpu.VMEM((WIDTH, rows), F32),
                 pltpu.VMEM((WIDTH, rows), BF16),
                 pltpu.VMEM((3, members, FEAT, rows), BF16),
                 pltpu.VMEM((members, PAIRS, AUG_ROWS, rows), BF16),
-                pltpu.VMEM((8, rows), jnp.int32),
-                pltpu.VMEM((members, 8, rows), jnp.int32),
+                pltpu.VMEM((1, rows), jnp.int32),
+                pltpu.VMEM((members, 1, rows), jnp.int32),
                 pltpu.VMEM((2 * HEADS, rows), F32),
                 pltpu.VMEM((total, rows), F32),
                 pltpu.VMEM((PAIRS, total, 2 * rows), F32),
@@ -586,7 +624,9 @@
                 pltpu.VMEM((8, 128), F32),
                 pltpu.VMEM((members, 8, 128), F32),
                 pltpu.VMEM((8, 128), F32),
-                pltpu.VMEM((groups, 8, 128), F32),
+                pltpu.VMEM((8, 128), F32),
+                pltpu.VMEM((8, 128), F32),
+                pltpu.VMEM((outer, 8, 128), F32),
                 dma((6,)),
                 dma((2 * PAIRS + 1,)),
                 dma((2 * PAIRS + 1,)),
@@ -602,8 +642,9 @@
                 dma((mine, 2)),
                 dma((1,)),
                 dma((1,)),
-                dma((3,)),
-                dma((3,)),
+                dma((4,)),
+                dma((4,)),
+                pltpu.SemaphoreType.REGULAR((2,)),
             ],
             compiler_params=pltpu.CompilerParams(collective_id=0, has_side_effects=True, vmem_limit_bytes=48000000),
             name="sublayer",

time: 33.5 us -> 32.7 us (0.976)
  Pallas kernels: 32 us -> 31.3 us
    pallas_call x1, Pallas kernels: 30.9 us -> 30.2 us  [local(): pl.pallas_call(functools.partial(kernel, members, groups), out_shape=(jax...]
where the time goes in v2:
time: 32.7 us; the launch traced here: 32.6 us
  Pallas kernels  31.3 us (96%)
  between operations  1.29 us (4%)
    pallas_call x1, Pallas kernels, local(): pl.pallas_call(functools.partial(kernel, members, groups), out_shape=(jax...  30.2 us
    pallas_call x1, Pallas kernels, local(): pl.pallas_call(functools.partial(scale_kernel, groups * total, total), ou...  1.09 us

profile of v2, /device:TPU:0, one launch (start us, length us, event | category | flops | bytes accessed | tf_op | source)
XLA Modules:
  0.0 32.6 jit_solution(6884658081941208257)
XLA Ops:
  1.3 30.2 %sublayer.1 = (f32[576,128]{1,0:T(8,128)S(1)}, f32[576,128]{1,0:T(8,128)S(1)}, f32[576,128]{1,0:T(8,128)S(1)}, f32[144,144]{1,0:T(8,128)S(1)}, f32[8,128]{1,0:T(8,128)S(1)}) custom-call(s32[1]{0:T(128)S(6)} %copy.12.len_ref, s32[1,128]{1,0:T(1,128)} %seg_hbm.1, bf16[576,128]{1,0:T(8,128)(2,1)} %bitcast.21, bf16[576,128]{1,0:T(8,128)(2,1)} %bitcast.22, ...), custom_call_target="tpu_custom_call" | custom-call | tf_op jit(solution)/shard_map/sublayer/pallas_call | solution.py:593
  31.5 1.1 %scale.1 = (f32[576,128]{1,0:T(8,128)}, f32[576,128]{1,0:T(8,128)}, f32[576,128]{1,0:T(8,128)}, f32[144,144]{1,0:T(8,128)}, f32[1,1]{1,0:T(1,128)}) custom-call(f32[8,128]{1,0:T(8,128)S(1)} %get-tuple-element.15.sum_ref, f32[576,128]{1,0:T(8,128)S(1)} %get-tuple-element.16.dq_ref, f32[576,128]{1,0:T(8,128)S(1)} %get-tuple-element.17.dk_ref, ...), custom_call_target="tpu_custom_call" | custom-call | tf_op jit(solution)/shard_map/scale/pallas_call | solution.py:652

commit v3 on v2

--- a/solution.py
+++ b/solution.py
@@ -77,8 +77,9 @@
     bias_ref,
     prob_ref,
     at_ref,
-    dt_own,
-    dt_all,
+    tt_own,
+    tt_all,
+    other_ref,
     u_own,
     y_all,
     z_own,
@@ -98,8 +99,8 @@
     g_send,
     at_send,
     at_recv,
-    dt_send,
-    dt_recv,
+    tt_send,
+    tt_recv,
     y_send,
     y_recv,
     z_send,
@@ -112,7 +113,6 @@
     chips = members // 2
     outer = groups // 2
     mine = outer // 2
-    half = mine // 2
     share, features, main, rest, main_rows, tiles, unit_rows = unit_layout(members, groups)
     rest_rows = pad16(rest)
     me = lax.axis_index("patch")
@@ -122,6 +122,7 @@
     partner = chip * 2 + 1 - core
     across = step_a * 2 + 1 - step_b
     slot = step_b * 2 + core
+    job = (core + chip) % 2
 
     def patch_peer(shift):
         return lax.rem(me + shift, members)
@@ -209,13 +210,13 @@
 
     def spread(part, index, send, away, near):
         for shift in range(1, chips):
-            copy(part, part, send, away.at[index], (dp, far(shift) * 2 + core)).start()
+            copy(part, part, send, away.at[index], (dp, far(shift) * 2 + 1 - core)).start()
         copy(part, part, send, near.at[index], (dp, partner)).start()
 
     def relay_parts(part_at, span_at, index, send, away, near):
-        received(part_at(far(1) * 2 + core) if chips == 2 else span_at(chips - 1), away.at[index])
+        received(part_at(far(1) * 2 + 1 - core) if chips == 2 else span_at(chips - 1), away.at[index])
         for shift in range(1, chips):
-            part = part_at(far(shift) * 2 + core)
+            part = part_at(far(shift) * 2 + 1 - core)
             copy(part, part, send, near.at[index], (dp, partner)).start()
 
     def kvq_span(array, pair, count):
@@ -296,10 +297,28 @@
     norm_picker, delta_picker = picker(0), picker(6)
 
     loads[5].wait()
-    acc_ref[...] = -(t_ref[...].astype(F32).T)
+    target = t_ref[...].astype(F32).T
+    acc_ref[...] = -target
+    for z in range(outer):
+        for side in (0, 1):
+            low = (z * 2 + side) * share
+            tt_own[side, z] = target[low : low + share].astype(BF16)
+    peers = ((1 - step_b, core), (1 - step_b, 1 - core), (step_b, 1 - core))
+    for side, to in peers:
+        copy(
+            tt_own.at[side, pl.ds((to + chip) % 2 * mine, mine)],
+            tt_all.at[slot],
+            tt_send.at[0],
+            tt_recv.at[0],
+            (step_a * 2 + side, chip * 2 + to),
+        ).start()
+    for i in range(mine):
+        tt_all[slot, i] = tt_own[step_b, job * mine + i]
     loads[4].wait()
     for pair in range(PAIRS):
-        wt_ref[pair] = w_ref[PAIR_ROWS * pair : PAIR_ROWS * (pair + 1), :].astype(F32).T.astype(BF16)
+        turned = w_ref[PAIR_ROWS * pair : PAIR_ROWS * (pair + 1), :].astype(F32).T
+        for block in range(groups):
+            wt_ref[pair, block] = turned[block * share : (block + 1) * share].astype(BF16)
     u_own[:, :, main_rows:, :] = jnp.zeros((mine, members, unit_rows - main_rows, LANES), BF16)
 
     length = len_ref[0]
@@ -338,12 +357,17 @@
             kvq_relay(KEY, pair + 1)
         kvq_finish(VALUE, pair)
         accum = nn(whole(VALUE, pair), probs.astype(BF16))
-        attn_pair = merged(accum / denom).astype(BF16)
+        attn_pair = jnp.where(own_live, merged(accum / denom), 0.0).astype(BF16)
         at_ref[slot, PAIR_ROWS * pair : PAIR_ROWS * (pair + 1), :] = attn_pair
         part = at_ref.at[slot, rows_of(pair)]
-        copy(part, part, at_send.at[0], at_recv.at[0], (across, me)).start()
-        copy(part, part, at_send.at[0], at_recv.at[1], (dp, partner)).start()
-        acc_ref[...] += nn(wt_ref[pair], attn_pair)
+        for side, to in peers:
+            arrival = at_recv.at[pair // (PAIRS - 1)]
+            copy(part, part, at_send.at[0], arrival, (step_a * 2 + side, chip * 2 + to)).start()
+        if share % 16 == 0:
+            acc_ref[...] += nn(wt_ref[pair].reshape(WIDTH, PAIR_ROWS), attn_pair)
+        else:
+            for block in range(groups):
+                acc_ref[block * share : (block + 1) * share, :] += nn(wt_ref[pair, block], attn_pair)
         if pair == 2 and outer > 2:
             wave_wait()
             if outer > 3:
@@ -352,21 +376,10 @@
     error = jnp.where(own_live, acc_ref[...], 0.0)
     dout = (2.0 * error).astype(BF16)
     dout_ref[...] = dout
-    for z in range(outer):
-        for side in (0, 1):
-            low = (z * 2 + side) * share
-            dt_own[side, z] = dout[low : low + share]
-    for chunk in (0, 1):
-        for side, to in ((1 - step_b, core), (1 - step_b, 1 - core), (step_b, 1 - core)):
-            copy(
-                dt_own.at[side, pl.ds(to * mine + chunk * half, half)],
-                dt_all.at[pl.ds(chunk * half, half), slot],
-                dt_send.at[0],
-                dt_recv.at[chunk],
-                (step_a * 2 + side, chip * 2 + to),
-            ).start()
-    for i in range(mine):
-        dt_all[i, slot] = dt_own[step_b, core * mine + i]
+    loss_part = jnp.sum(jnp.sum(error * error, axis=0, keepdims=True), axis=1, keepdims=True)
+    tile_own[...] = jnp.broadcast_to(loss_part, tile_own.shape)
+    small(1, tile_own, tile_all)
+    tile_all[me] = tile_own[...]
 
     def terms(value):
         first = value.astype(BF16).astype(F32)
@@ -389,11 +402,6 @@
         g_ref[me, pair, PAIR_ROWS:, :] = jnp.concatenate(lines, axis=0).astype(BF16)
         g_spread(pair)
 
-    loss_part = jnp.sum(jnp.sum(error * error, axis=0, keepdims=True), axis=1, keepdims=True)
-    tile_own[...] = jnp.broadcast_to(loss_part, tile_own.shape)
-    small(1, tile_own, tile_all)
-    tile_all[me] = tile_own[...]
-
     def query_pass(pair):
         low = HEADS + 2 * pair
         delta = jnp.concatenate([stat_ref[low : low + 1, :], stat_ref[low + 1 : low + 2, :]], axis=1)
@@ -418,16 +426,32 @@
         dscores = (probs * dprobs).astype(BF16)
         dk_ref[PAIR_ROWS * pair : PAIR_ROWS * (pair + 1), :] = merged(nn(queries, dscores)) * score_scale
 
-    def weight_part(chunk):
-        received(dt_all.at[pl.ds(chunk * half, half), pl.ds(0, 3)], dt_recv.at[chunk])
+    def attention(pair):
+        low = PAIR_ROWS * pair
+        return jnp.concatenate([at_ref[s, low : low + PAIR_ROWS, :] for s in range(4)], axis=1)
+
+    def weight_start():
+        received(tt_all.at[pl.ds(0, 3)], tt_recv.at[0])
+        received(at_ref.at[pl.ds(0, 3), pl.ds(0, FEAT - PAIR_ROWS)], at_recv.at[0])
+        for i in range(mine):
+            block = (job * mine + i) * 2 + step_b
+            value = -jnp.concatenate([tt_all[s, i].astype(F32) for s in range(4)], axis=1)
+            for pair in range(PAIRS - 1):
+                value = value + nn(wt_ref[pair, block], attention(pair))
+            other_ref[i] = value
+
+    def weight_part():
+        received(at_ref.at[pl.ds(0, 3), rows_of(PAIRS - 1)], at_recv.at[1])
         attn = jnp.concatenate([at_ref[s] for s in range(4)], axis=1)
         if main:
             attn_main = jnp.concatenate([attn[p * features : p * features + main] for p in range(members)], axis=0)
             attn_rest = jnp.concatenate([attn[p * features + main : (p + 1) * features] for p in range(members)], axis=0)
         else:
             attn_rest = attn
-        for i in range(chunk * half, (chunk + 1) * half):
-            grads = jnp.concatenate([dt_all[i, s] for s in range(4)], axis=1)
+        for i in range(mine):
+            block = (job * mine + i) * 2 + step_b
+            value = other_ref[i] + nn(wt_ref[PAIRS - 1, block], attention(PAIRS - 1))
+            grads = (2.0 * value).astype(BF16)
             if main:
                 part_main = nt(grads, attn_main).astype(BF16)
             part_rest = nt(attn_rest, grads)
@@ -441,12 +465,13 @@
                     u_own[i, p, low : low + rest, :wide] = piece
             for to in (0, 1):
                 for shift in range(1, chips):
+                    away = far(shift)
                     copy(
-                        u_own.at[i, far(shift) * 2 + to],
+                        u_own.at[i, away * 2 + to],
                         y_all.at[i, to, chip],
                         y_send.at[0],
                         y_recv.at[i, to],
-                        (dp, far(shift) * 2 + core),
+                        (dp, away * 2 + (job + away) % 2),
                     ).start()
 
     def weight_sum(i, to):
@@ -455,8 +480,8 @@
         for shift in range(1, chips):
             value = value + y_all[i, to, far(shift)].astype(F32)
         z_own[i, to] = value.astype(BF16)
-        target = core * mine + i
-        stays = jnp.logical_and(target == step_a, core == to)
+        owner = job * mine + i
+        stays = jnp.logical_and(owner == step_a, core == to)
 
         @pl.when(stays)
         def _():
@@ -469,7 +494,7 @@
                 z_all.at[step_a],
                 z_send.at[0],
                 z_recv.at[0],
-                (target * 2 + step_b, chip * 2 + to),
+                (owner * 2 + step_b, chip * 2 + to),
             ).start()
 
     for hops in range(4, outer + 1):
@@ -477,20 +502,11 @@
         if hops < outer:
             wave_start()
     kvq_relay(QUERY)
-    received(at_ref.at[0], at_recv.at[0])
-    part = at_ref.at[(1 - step_b) * 2 + core]
-    copy(part, part, at_send.at[0], at_recv.at[1], (dp, partner)).start()
     query_pass(0)
+    weight_start()
     g_relay(0)
     query_pass(1)
     g_relay(1)
-    received(at_ref.at[pl.ds(0, 2)], at_recv.at[1])
-    weight_part(0)
-    g_relay(2)
-    query_pass(2)
-    weight_part(1)
-    g_relay(3)
-
     received(tile_all.at[pl.ds(0, members - 1)], small_recv.at[1])
     pack_loss = tile_all[0]
     for j in range(1, members):
@@ -498,20 +514,23 @@
     tile_lane = lax.broadcasted_iota(jnp.int32, pack_loss.shape, 1)
     pair_own[...] = jnp.where(tile_lane == 0, pack_loss, length.astype(F32))
     copy(pair_own, pair_all, small_send.at[3], small_recv.at[3], (across, me)).start()
-
+    weight_part()
+    g_relay(2)
+    query_pass(2)
+    g_relay(3)
     query_pass(3)
+    received(pair_all, small_recv.at[3])
+    sum_own[...] = pair_own[...] + pair_all[...]
+    for shift in range(1, outer):
+        to = outer_peer(shift) * 2 + step_b
+        copy(sum_own, sum_all.at[step_a], small_send.at[2], small_recv.at[2], (to, me)).start()
+    sum_all[step_a] = sum_own[...]
     kvq_finish(QUERY)
     key_pass(0)
     units = [(i, to) for i in range(mine) for to in (0, 1)]
     quarter = len(units) // 4
     for i, to in units[: 2 * quarter]:
         weight_sum(i, to)
-    received(pair_all, small_recv.at[3])
-    sum_own[...] = pair_own[...] + pair_all[...]
-    for shift in range(1, outer):
-        to = outer_peer(shift) * 2 + step_b
-        copy(sum_own, sum_all.at[step_a], small_send.at[2], small_recv.at[2], (to, me)).start()
-    sum_all[step_a] = sum_own[...]
     key_pass(1)
     for i, to in units[2 * quarter : 3 * quarter]:
         weight_sum(i, to)
@@ -529,14 +548,14 @@
     sent(kvq_ref.at[:, pl.ds(0, members - 1)], kvq_send.at[0])
     sent(g_ref.at[pl.ds(0, members - 1)], g_send.at[0])
     sent(at_ref.at[pl.ds(0, 3)], at_send.at[0])
-    sent(dt_all.at[:, pl.ds(0, 3)], dt_send.at[0])
+    sent(tt_all.at[pl.ds(0, 3)], tt_send.at[0])
     sent(y_all.at[:, :, pl.ds(0, chips - 1)], y_send.at[0])
     sent(seg_all.at[pl.ds(0, members - 1)], small_send.at[0])
     sent(tile_all.at[pl.ds(0, members - 1)], small_send.at[1])
     sent(sum_all.at[pl.ds(0, outer - 1)], small_send.at[2])
     sent(pair_all, small_send.at[3])
 
-    collects = core == step_a // mine
+    collects = job == step_a // mine
 
     @pl.when(collects)
     def _():
@@ -604,7 +623,7 @@
             scratch_shapes=[
                 pltpu.VMEM((FEAT, WIDTH), BF16),
                 pltpu.VMEM((rows, WIDTH), BF16),
-                pltpu.VMEM((PAIRS, WIDTH, PAIR_ROWS), BF16),
+                pltpu.VMEM((PAIRS, groups, share, PAIR_ROWS), BF16),
                 pltpu.VMEM((WIDTH, rows), F32),
                 pltpu.VMEM((WIDTH, rows), BF16),
                 pltpu.VMEM((3, members, FEAT, rows), BF16),
@@ -616,7 +635,8 @@
                 pltpu.VMEM((PAIRS, total, 2 * rows), F32),
                 pltpu.VMEM((4, FEAT, rows), BF16),
                 pltpu.VMEM((2, outer, share, rows), BF16),
-                pltpu.VMEM((mine, 4, share, rows), BF16),
+                pltpu.VMEM((4, mine, share, rows), BF16),
+                pltpu.VMEM((mine, share, 4 * rows), F32),
                 pltpu.VMEM((mine, members, unit_rows, LANES), BF16),
                 pltpu.VMEM((mine, 2, chips, unit_rows, LANES), BF16),
                 pltpu.VMEM((mine, 2, unit_rows, LANES), BF16),
@@ -637,7 +657,7 @@
                 dma((1,)),
                 dma((2,)),
                 dma((1,)),
-                dma((2,)),
+                dma((1,)),
                 dma((1,)),
                 dma((mine, 2)),
                 dma((1,)),

time: 32.7 us -> 31.4 us (0.960)
  Pallas kernels: 31.3 us -> 29.9 us
    pallas_call x1, Pallas kernels: 30.2 us -> 28.8 us  [local(): pl.pallas_call(functools.partial(kernel, members, groups), out_shape=(jax...]
where the time goes in v3:
time: 31.4 us; the launch traced here: 31.2 us
  Pallas kernels  29.9 us (95%)
  between operations  1.29 us (4%)
    pallas_call x1, Pallas kernels, local(): pl.pallas_call(functools.partial(kernel, members, groups), out_shape=(jax...  28.8 us
    pallas_call x1, Pallas kernels, local(): pl.pallas_call(functools.partial(scale_kernel, groups * total, total), ou...  1.09 us

profile of v3, /device:TPU:0, one launch (start us, length us, event | category | flops | bytes accessed | tf_op | source)
XLA Modules:
  0.0 31.2 jit_solution(4087971039262532349)
XLA Ops:
  1.3 28.8 %sublayer.1 = (f32[576,128]{1,0:T(8,128)S(1)}, f32[576,128]{1,0:T(8,128)S(1)}, f32[576,128]{1,0:T(8,128)S(1)}, f32[144,144]{1,0:T(8,128)S(1)}, f32[8,128]{1,0:T(8,128)S(1)}) custom-call(s32[1]{0:T(128)S(6)} %copy.12.len_ref, s32[1,128]{1,0:T(1,128)} %seg_hbm.1, bf16[576,128]{1,0:T(8,128)(2,1)} %bitcast.21, bf16[576,128]{1,0:T(8,128)(2,1)} %bitcast.22, ...), custom_call_target="tpu_custom_call" | custom-call | tf_op jit(solution)/shard_map/sublayer/pallas_call | solution.py:612
  30.1 1.1 %scale.1 = (f32[576,128]{1,0:T(8,128)}, f32[576,128]{1,0:T(8,128)}, f32[576,128]{1,0:T(8,128)}, f32[144,144]{1,0:T(8,128)}, f32[1,1]{1,0:T(1,128)}) custom-call(f32[8,128]{1,0:T(8,128)S(1)} %get-tuple-element.15.sum_ref, f32[576,128]{1,0:T(8,128)S(1)} %get-tuple-element.16.dq_ref, f32[576,128]{1,0:T(8,128)S(1)} %get-tuple-element.17.dk_ref, ...), custom_call_target="tpu_custom_call" | custom-call | tf_op jit(solution)/shard_map/scale/pallas_call | solution.py:672

commit v4 on v3

--- a/solution.py
+++ b/solution.py
@@ -325,6 +325,7 @@
     lane_position = lax.broadcasted_iota(jnp.int32, (1, rows), 1)
     own_live = me * rows + lane_position < length
     own_group = jnp.where(own_live, seg_own[...], -1).astype(F32)
+    kvq_relay(KEY, 0)
     received(seg_all.at[pl.ds(0, members - 1)], small_recv.at[0])
     for j in range(members):
         group = jnp.where(j * rows + lane_position < length, seg_all[j], -1).astype(F32)
@@ -338,8 +339,13 @@
         bias = bias_ref[...]
         return scores * log_scale + jnp.concatenate([bias, bias], axis=1)
 
-    denoms = []
-    kvq_relay(KEY, 0)
+    def projected(pair):
+        attn_pair = at_ref[slot, PAIR_ROWS * pair : PAIR_ROWS * (pair + 1), :]
+        if share % 16 == 0:
+            return nn(wt_ref[pair].reshape(WIDTH, PAIR_ROWS), attn_pair)
+        return jnp.concatenate([nn(wt_ref[pair, block], attn_pair) for block in range(groups)], axis=0)
+
+    inverses = []
     for pair in range(PAIRS):
         kvq_finish(KEY, pair)
         kvq_relay(VALUE, pair)
@@ -352,28 +358,26 @@
         for side in (0, 1):
             head = 2 * pair + side
             stat_ref[head : head + 1, :] = log_norm[:, side * rows : (side + 1) * rows]
-        denoms.append(denom)
+        inverse = 1.0 / denom
+        inverses.append(inverse)
         if pair + 1 < PAIRS:
             kvq_relay(KEY, pair + 1)
+        if pair:
+            acc_ref[...] += projected(pair - 1)
         kvq_finish(VALUE, pair)
-        accum = nn(whole(VALUE, pair), probs.astype(BF16))
-        attn_pair = jnp.where(own_live, merged(accum / denom), 0.0).astype(BF16)
+        accum = nn(whole(VALUE, pair), probs.astype(BF16)) * inverse
+        attn_pair = jnp.where(own_live, merged(accum), 0.0).astype(BF16)
         at_ref[slot, PAIR_ROWS * pair : PAIR_ROWS * (pair + 1), :] = attn_pair
         part = at_ref.at[slot, rows_of(pair)]
         for side, to in peers:
             arrival = at_recv.at[pair // (PAIRS - 1)]
             copy(part, part, at_send.at[0], arrival, (step_a * 2 + side, chip * 2 + to)).start()
-        if share % 16 == 0:
-            acc_ref[...] += nn(wt_ref[pair].reshape(WIDTH, PAIR_ROWS), attn_pair)
-        else:
-            for block in range(groups):
-                acc_ref[block * share : (block + 1) * share, :] += nn(wt_ref[pair, block], attn_pair)
-        if pair == 2 and outer > 2:
+        if pair == 1 and outer > 2:
             wave_wait()
             if outer > 3:
                 wave_start()
 
-    error = jnp.where(own_live, acc_ref[...], 0.0)
+    error = jnp.where(own_live, acc_ref[...] + projected(PAIRS - 1), 0.0)
     dout = (2.0 * error).astype(BF16)
     dout_ref[...] = dout
     loss_part = jnp.sum(jnp.sum(error * error, axis=0, keepdims=True), axis=1, keepdims=True)
@@ -407,7 +411,7 @@
         delta = jnp.concatenate([stat_ref[low : low + 1, :], stat_ref[low + 1 : low + 2, :]], axis=1)
         grad = g_ref[me, pair, :PAIR_ROWS, :]
         dprobs = tn(whole(VALUE, pair), stacked(grad))
-        dscores = prob_ref[pair] * (1.0 / denoms[pair]) * (dprobs - delta)
+        dscores = prob_ref[pair] * inverses[pair] * (dprobs - delta)
         value = nn(whole(KEY, pair), dscores.astype(BF16))
         dq_ref[PAIR_ROWS * pair : PAIR_ROWS * (pair + 1), :] = merged(value) * score_scale
 
@@ -440,32 +444,38 @@
                 value = value + nn(wt_ref[pair, block], attention(pair))
             other_ref[i] = value
 
+    def weight_blocks(away, blocks, grads, attn, span):
+        if main:
+            attn_main = jnp.concatenate([attn[p * features : p * features + main] for p in range(span)], axis=0)
+            attn_rest = jnp.concatenate([attn[p * features + main : (p + 1) * features] for p in range(span)], axis=0)
+            part_main = nt(grads, attn_main).astype(BF16)
+        else:
+            attn_rest = attn
+        part_rest = nt(attn_rest, grads)
+        for place, i in enumerate(blocks):
+            for p in range(span):
+                if main:
+                    u_own[i, away + p, :share, :] = part_main[place * share : (place + 1) * share, p * main : (p + 1) * main]
+                for t in range(tiles):
+                    wide = min(share - t * LANES, LANES)
+                    first = place * share + t * LANES
+                    low = main_rows + t * rest_rows
+                    piece = part_rest[p * rest : (p + 1) * rest, first : first + wide]
+                    u_own[i, away + p, low : low + rest, :wide] = piece.astype(BF16)
+
     def weight_part():
         received(at_ref.at[pl.ds(0, 3), rows_of(PAIRS - 1)], at_recv.at[1])
-        attn = jnp.concatenate([at_ref[s] for s in range(4)], axis=1)
-        if main:
-            attn_main = jnp.concatenate([attn[p * features : p * features + main] for p in range(members)], axis=0)
-            attn_rest = jnp.concatenate([attn[p * features + main : (p + 1) * features] for p in range(members)], axis=0)
-        else:
-            attn_rest = attn
+        last = attention(PAIRS - 1)
+        grads = []
         for i in range(mine):
             block = (job * mine + i) * 2 + step_b
-            value = other_ref[i] + nn(wt_ref[PAIRS - 1, block], attention(PAIRS - 1))
-            grads = (2.0 * value).astype(BF16)
-            if main:
-                part_main = nt(grads, attn_main).astype(BF16)
-            part_rest = nt(attn_rest, grads)
-            for p in range(members):
-                if main:
-                    u_own[i, p, :share, :] = part_main[:, p * main : (p + 1) * main]
-                for t in range(tiles):
-                    wide = min(share - t * LANES, LANES)
-                    piece = part_rest[p * rest : (p + 1) * rest, t * LANES : t * LANES + wide].astype(BF16)
-                    low = main_rows + t * rest_rows
-                    u_own[i, p, low : low + rest, :wide] = piece
-            for to in (0, 1):
-                for shift in range(1, chips):
-                    away = far(shift)
+            value = other_ref[i] + nn(wt_ref[PAIRS - 1, block], last)
+            grads.append((2.0 * value).astype(BF16))
+
+        def send(shift):
+            away = far(shift)
+            for i in range(mine):
+                for to in (0, 1):
                     copy(
                         u_own.at[i, away * 2 + to],
                         y_all.at[i, to, chip],
@@ -473,6 +483,21 @@
                         y_recv.at[i, to],
                         (dp, away * 2 + (job + away) % 2),
                     ).start()
+
+        if share % 16 == 0 and features % 16 == 0:
+            every = jnp.concatenate(grads, axis=0)
+            for shift in [*range(1, chips), 0]:
+                low = pl.multiple_of(far(shift) * 2 * features, 16)
+                attn = jnp.concatenate([at_ref[s, pl.ds(low, 2 * features), :] for s in range(4)], axis=1)
+                weight_blocks(far(shift) * 2, range(mine), every, attn, 2)
+                if shift:
+                    send(shift)
+        else:
+            attn = jnp.concatenate([at_ref[s] for s in range(4)], axis=1)
+            for i in range(mine):
+                weight_blocks(0, [i], grads[i], attn, members)
+            for shift in range(1, chips):
+                send(shift)
 
     def weight_sum(i, to):
         received(y_all.at[i, to, pl.ds(0, chips - 1)], y_recv.at[i, to])
@@ -504,9 +529,7 @@
     kvq_relay(QUERY)
     query_pass(0)
     weight_start()
-    g_relay(0)
     query_pass(1)
-    g_relay(1)
     received(tile_all.at[pl.ds(0, members - 1)], small_recv.at[1])
     pack_loss = tile_all[0]
     for j in range(1, members):
@@ -515,29 +538,26 @@
     pair_own[...] = jnp.where(tile_lane == 0, pack_loss, length.astype(F32))
     copy(pair_own, pair_all, small_send.at[3], small_recv.at[3], (across, me)).start()
     weight_part()
+    g_relay(0)
+    g_relay(1)
+    query_pass(2)
     g_relay(2)
-    query_pass(2)
+    query_pass(3)
     g_relay(3)
-    query_pass(3)
-    received(pair_all, small_recv.at[3])
-    sum_own[...] = pair_own[...] + pair_all[...]
-    for shift in range(1, outer):
-        to = outer_peer(shift) * 2 + step_b
-        copy(sum_own, sum_all.at[step_a], small_send.at[2], small_recv.at[2], (to, me)).start()
-    sum_all[step_a] = sum_own[...]
     kvq_finish(QUERY)
-    key_pass(0)
     units = [(i, to) for i in range(mine) for to in (0, 1)]
-    quarter = len(units) // 4
-    for i, to in units[: 2 * quarter]:
-        weight_sum(i, to)
-    key_pass(1)
-    for i, to in units[2 * quarter : 3 * quarter]:
-        weight_sum(i, to)
-    key_pass(2)
-    for i, to in units[3 * quarter :]:
-        weight_sum(i, to)
-    key_pass(3)
+    quarter = len(units) // PAIRS
+    for pair in range(PAIRS):
+        key_pass(pair)
+        for i, to in units[pair * quarter : (pair + 1) * quarter]:
+            weight_sum(i, to)
+        if pair == 0:
+            received(pair_all, small_recv.at[3])
+            sum_own[...] = pair_own[...] + pair_all[...]
+            for shift in range(1, outer):
+                to = outer_peer(shift) * 2 + step_b
+                copy(sum_own, sum_all.at[step_a], small_send.at[2], small_recv.at[2], (to, me)).start()
+            sum_all[step_a] = sum_own[...]
 
     received(sum_all.at[pl.ds(0, outer - 1)], small_recv.at[2])
     totals = sum_all[0]

time: 31.4 us -> 30.1 us (0.959); the launches traced: 31.2 us -> 29.5 us
  Pallas kernels: 29.9 us -> 28.2 us
    pallas_call x1, Pallas kernels: 28.8 us -> 27.1 us  [local(): pl.pallas_call(functools.partial(kernel, members, groups), out_shape=(jax...]
where the time goes in v4:
time: 30.1 us; the launch traced here: 29.5 us
  Pallas kernels  28.2 us (94%)
  between operations  1.29 us (4%)
    pallas_call x1, Pallas kernels, local(): pl.pallas_call(functools.partial(kernel, members, groups), out_shape=(jax...  27.1 us
    pallas_call x1, Pallas kernels, local(): pl.pallas_call(functools.partial(scale_kernel, groups * total, total), ou...  1.09 us

profile of v4, /device:TPU:0, one launch (start us, length us, event | category | flops | bytes accessed | tf_op | source)
XLA Modules:
  0.0 29.5 jit_solution(5270843441072611000)
XLA Ops:
  1.3 27.1 %sublayer.1 = (f32[576,128]{1,0:T(8,128)S(1)}, f32[576,128]{1,0:T(8,128)S(1)}, f32[576,128]{1,0:T(8,128)S(1)}, f32[144,144]{1,0:T(8,128)S(1)}, f32[8,128]{1,0:T(8,128)S(1)}) custom-call(s32[1]{0:T(128)S(6)} %copy.12.len_ref, s32[1,128]{1,0:T(1,128)} %seg_hbm.1, bf16[576,128]{1,0:T(8,128)(2,1)} %bitcast.21, bf16[576,128]{1,0:T(8,128)(2,1)} %bitcast.22, ...), custom_call_target="tpu_custom_call" | custom-call | tf_op jit(solution)/shard_map/sublayer/pallas_call | solution.py:632
  28.4 1.1 %scale.1 = (f32[576,128]{1,0:T(8,128)}, f32[576,128]{1,0:T(8,128)}, f32[576,128]{1,0:T(8,128)}, f32[144,144]{1,0:T(8,128)}, f32[1,1]{1,0:T(1,128)}) custom-call(f32[8,128]{1,0:T(8,128)S(1)} %get-tuple-element.15.sum_ref, f32[576,128]{1,0:T(8,128)S(1)} %get-tuple-element.16.dq_ref, f32[576,128]{1,0:T(8,128)S(1)} %get-tuple-element.17.dk_ref, ...), custom_call_target="tpu_custom_call" | custom-call | tf_op jit(solution)/shard_map/scale/pallas_call | solution.py:692

commit v5 on v4

--- a/solution.py
+++ b/solution.py
@@ -240,33 +240,43 @@
     def kvq_finish(array, pair=0):
         received(kvq_span(array, pair, chips), near_sem.at[kvq_index(array, pair)])
 
-    def g_spread(pair):
-        spread(g_ref.at[me, pair], pair, g_send.at[0], g_far, g_near)
-
-    def g_relay(pair):
+    def g_part(owner, part):
+        return g_ref.at[owner, pl.ds(2 * part, 2)]
+
+    def g_span(part, count):
+        return g_ref.at[pl.ds(0, count), pl.ds(2 * part, 2)]
+
+    def g_spread(part):
+        spread(g_part(me, part), part, g_send.at[0], g_far, g_near)
+
+    def g_relay(part):
         relay_parts(
-            lambda owner: g_ref.at[owner, pair],
-            lambda count: g_ref.at[pl.ds(0, count), pair],
-            pair,
+            lambda owner: g_part(owner, part),
+            lambda count: g_span(part, count),
+            part,
             g_send.at[0],
             g_far,
             g_near,
         )
 
-    def g_finish(pair):
-        received(g_ref.at[pl.ds(0, chips), pair], g_near.at[pair])
+    def g_finish(part):
+        received(g_span(part, chips), g_near.at[part])
 
     def small(index, own_ref, everyone):
         for shift in range(1, members):
             copy(own_ref, everyone.at[me], small_send.at[index], small_recv.at[index], (dp, patch_peer(shift))).start()
 
-    for load in (loads[2], loads[0], loads[1], loads[3]):
-        load.wait()
+    loads[0].wait()
     pl.semaphore_wait(barrier, greeted)
+    kvq_spread(KEY, 0)
+    loads[2].wait()
     small(0, seg_own, seg_all)
-    for pair in range(PAIRS):
+    loads[1].wait()
+    kvq_spread(VALUE, 0)
+    for pair in range(1, PAIRS):
         kvq_spread(KEY, pair)
         kvq_spread(VALUE, pair)
+    loads[3].wait()
     kvq_spread(QUERY)
     wave_start()
     seg_all[me] = seg_own[...]
@@ -404,7 +414,8 @@
             lines += terms(delta)
         lines.append(jnp.zeros((STAT_ROWS - 12, rows), F32))
         g_ref[me, pair, PAIR_ROWS:, :] = jnp.concatenate(lines, axis=0).astype(BF16)
-        g_spread(pair)
+        if pair % 2:
+            g_spread(pair // 2)
 
     def query_pass(pair):
         low = HEADS + 2 * pair
@@ -416,7 +427,8 @@
         dq_ref[PAIR_ROWS * pair : PAIR_ROWS * (pair + 1), :] = merged(value) * score_scale
 
     def key_pass(pair):
-        g_finish(pair)
+        if pair % 2 == 0:
+            g_finish(pair // 2)
         queries = whole(QUERY, pair)
         grads = jnp.concatenate([g_ref[j, pair] for j in range(members)], axis=1)
         stats = grads[PAIR_ROWS:]
@@ -466,38 +478,41 @@
     def weight_part():
         received(at_ref.at[pl.ds(0, 3), rows_of(PAIRS - 1)], at_recv.at[1])
         last = attention(PAIRS - 1)
-        grads = []
-        for i in range(mine):
+
+        def grads_of(i):
             block = (job * mine + i) * 2 + step_b
-            value = other_ref[i] + nn(wt_ref[PAIRS - 1, block], last)
-            grads.append((2.0 * value).astype(BF16))
-
-        def send(shift):
+            return (2.0 * (other_ref[i] + nn(wt_ref[PAIRS - 1, block], last))).astype(BF16)
+
+        def send(i, shift):
             away = far(shift)
+            for to in (0, 1):
+                copy(
+                    u_own.at[i, away * 2 + to],
+                    y_all.at[i, to, chip],
+                    y_send.at[0],
+                    y_recv.at[i, to],
+                    (dp, away * 2 + (job + away) % 2),
+                ).start()
+
+        if share % 16 == 0 and features % 16 == 0:
+
+            def attn_of(shift):
+                low = pl.multiple_of(far(shift) * 2 * features, 16)
+                return jnp.concatenate([at_ref[s, pl.ds(low, 2 * features), :] for s in range(4)], axis=1)
+
+            grads = []
             for i in range(mine):
-                for to in (0, 1):
-                    copy(
-                        u_own.at[i, away * 2 + to],
-                        y_all.at[i, to, chip],
-                        y_send.at[0],
-                        y_recv.at[i, to],
-                        (dp, away * 2 + (job + away) % 2),
-                    ).start()
-
-        if share % 16 == 0 and features % 16 == 0:
-            every = jnp.concatenate(grads, axis=0)
-            for shift in [*range(1, chips), 0]:
-                low = pl.multiple_of(far(shift) * 2 * features, 16)
-                attn = jnp.concatenate([at_ref[s, pl.ds(low, 2 * features), :] for s in range(4)], axis=1)
-                weight_blocks(far(shift) * 2, range(mine), every, attn, 2)
-                if shift:
-                    send(shift)
+                grads.append(grads_of(i))
+                for shift in range(1, chips):
+                    weight_blocks(far(shift) * 2, [i], grads[i], attn_of(shift), 2)
+                    send(i, shift)
+            weight_blocks(chip * 2, range(mine), jnp.concatenate(grads, axis=0), attn_of(0), 2)
         else:
             attn = jnp.concatenate([at_ref[s] for s in range(4)], axis=1)
             for i in range(mine):
-                weight_blocks(0, [i], grads[i], attn, members)
-            for shift in range(1, chips):
-                send(shift)
+                weight_blocks(0, [i], grads_of(i), attn, members)
+                for shift in range(1, chips):
+                    send(i, shift)
 
     def weight_sum(i, to):
         received(y_all.at[i, to, pl.ds(0, chips - 1)], y_recv.at[i, to])
@@ -539,11 +554,15 @@
     copy(pair_own, pair_all, small_send.at[3], small_recv.at[3], (across, me)).start()
     weight_part()
     g_relay(0)
+    query_pass(2)
+    query_pass(3)
     g_relay(1)
-    query_pass(2)
-    g_relay(2)
-    query_pass(3)
-    g_relay(3)
+    received(pair_all, small_recv.at[3])
+    sum_own[...] = pair_own[...] + pair_all[...]
+    for shift in range(1, outer):
+        to = outer_peer(shift) * 2 + step_b
+        copy(sum_own, sum_all.at[step_a], small_send.at[2], small_recv.at[2], (to, me)).start()
+    sum_all[step_a] = sum_own[...]
     kvq_finish(QUERY)
     units = [(i, to) for i in range(mine) for to in (0, 1)]
     quarter = len(units) // PAIRS
@@ -551,13 +570,6 @@
         key_pass(pair)
         for i, to in units[pair * quarter : (pair + 1) * quarter]:
             weight_sum(i, to)
-        if pair == 0:
-            received(pair_all, small_recv.at[3])
-            sum_own[...] = pair_own[...] + pair_all[...]
-            for shift in range(1, outer):
-                to = outer_peer(shift) * 2 + step_b
-                copy(sum_own, sum_all.at[step_a], small_send.at[2], small_recv.at[2], (to, me)).start()
-            sum_all[step_a] = sum_own[...]
 
     received(sum_all.at[pl.ds(0, outer - 1)], small_recv.at[2])
     totals = sum_all[0]
@@ -671,8 +683,8 @@
                 dma((2 * PAIRS + 1,)),
                 dma((2 * PAIRS + 1,)),
                 dma((1,)),
-                dma((PAIRS,)),
-                dma((PAIRS,)),
+                dma((PAIRS // 2,)),
+                dma((PAIRS // 2,)),
                 dma((1,)),
                 dma((1,)),
                 dma((2,)),

time: 30.1 us -> 29.6 us (0.983)
  no operation moved by 1% of the time
where the time goes in v5:
time: 29.6 us; the launch traced here: 29.2 us
  Pallas kernels  27.9 us (94%)
  between operations  1.29 us (4%)
    pallas_call x1, Pallas kernels, local(): pl.pallas_call(functools.partial(kernel, members, groups), out_shape=(jax...  26.8 us
    pallas_call x1, Pallas kernels, local(): pl.pallas_call(functools.partial(scale_kernel, groups * total, total), ou...  1.09 us

profile of v5, /device:TPU:0, one launch (start us, length us, event | category | flops | bytes accessed | tf_op | source)
XLA Modules:
  0.0 29.2 jit_solution(1644068654074133112)
XLA Ops:
  1.3 26.8 %sublayer.1 = (f32[576,128]{1,0:T(8,128)S(1)}, f32[576,128]{1,0:T(8,128)S(1)}, f32[576,128]{1,0:T(8,128)S(1)}, f32[144,144]{1,0:T(8,128)S(1)}, f32[8,128]{1,0:T(8,128)S(1)}) custom-call(s32[1]{0:T(128)S(6)} %copy.12.len_ref, s32[1,128]{1,0:T(1,128)} %seg_hbm.1, bf16[576,128]{1,0:T(8,128)(2,1)} %bitcast.21, bf16[576,128]{1,0:T(8,128)(2,1)} %bitcast.22, ...), custom_call_target="tpu_custom_call" | custom-call | tf_op jit(solution)/shard_map/sublayer/pallas_call | solution.py:644
  28.1 1.1 %scale.1 = (f32[576,128]{1,0:T(8,128)}, f32[576,128]{1,0:T(8,128)}, f32[576,128]{1,0:T(8,128)}, f32[144,144]{1,0:T(8,128)}, f32[1,1]{1,0:T(1,128)}) custom-call(f32[8,128]{1,0:T(8,128)S(1)} %get-tuple-element.15.sum_ref, f32[576,128]{1,0:T(8,128)S(1)} %get-tuple-element.16.dq_ref, f32[576,128]{1,0:T(8,128)S(1)} %get-tuple-element.17.dk_ref, ...), custom_call_target="tpu_custom_call" | custom-call | tf_op jit(solution)/shard_map/scale/pallas_call | solution.py:704

commit v6 on v5

--- a/solution.py
+++ b/solution.py
@@ -22,6 +22,7 @@
 F32 = jnp.float32
 BF16 = jnp.bfloat16
 KEY, VALUE, QUERY = range(3)
+G_PARTS = ((0, 3), (3, 1))
 
 
 def nt(left, right):
@@ -68,7 +69,6 @@
     t_ref,
     wt_ref,
     acc_ref,
-    dout_ref,
     kvq_ref,
     g_ref,
     seg_own,
@@ -241,10 +241,10 @@
         received(kvq_span(array, pair, chips), near_sem.at[kvq_index(array, pair)])
 
     def g_part(owner, part):
-        return g_ref.at[owner, pl.ds(2 * part, 2)]
+        return g_ref.at[owner, pl.ds(*G_PARTS[part])]
 
     def g_span(part, count):
-        return g_ref.at[pl.ds(0, count), pl.ds(2 * part, 2)]
+        return g_ref.at[pl.ds(0, count), pl.ds(*G_PARTS[part])]
 
     def g_spread(part):
         spread(g_part(me, part), part, g_send.at[0], g_far, g_near)
@@ -357,8 +357,8 @@
 
     inverses = []
     for pair in range(PAIRS):
+        kvq_relay(VALUE, pair)
         kvq_finish(KEY, pair)
-        kvq_relay(VALUE, pair)
         scores = biased(tn(whole(KEY, pair), stacked(own(QUERY, pair))))
         row_max = jnp.max(scores, axis=0, keepdims=True)
         probs = jnp.exp2(scores - row_max)
@@ -379,9 +379,10 @@
         attn_pair = jnp.where(own_live, merged(accum), 0.0).astype(BF16)
         at_ref[slot, PAIR_ROWS * pair : PAIR_ROWS * (pair + 1), :] = attn_pair
         part = at_ref.at[slot, rows_of(pair)]
-        for side, to in peers:
-            arrival = at_recv.at[pair // (PAIRS - 1)]
-            copy(part, part, at_send.at[0], arrival, (step_a * 2 + side, chip * 2 + to)).start()
+        arrival = at_recv.at[pair // (PAIRS - 1)]
+        for to in (chip * 2 + chip % 2, chip * 2 + 1 - chip % 2):
+            copy(part, part, at_send.at[0], arrival, (across, to)).start()
+        copy(part, part, at_send.at[0], arrival, (dp, partner)).start()
         if pair == 1 and outer > 2:
             wave_wait()
             if outer > 3:
@@ -389,7 +390,6 @@
 
     error = jnp.where(own_live, acc_ref[...] + projected(PAIRS - 1), 0.0)
     dout = (2.0 * error).astype(BF16)
-    dout_ref[...] = dout
     loss_part = jnp.sum(jnp.sum(error * error, axis=0, keepdims=True), axis=1, keepdims=True)
     tile_own[...] = jnp.broadcast_to(loss_part, tile_own.shape)
     small(1, tile_own, tile_all)
@@ -401,7 +401,7 @@
         return [first, second, value - first - second]
 
     for pair in range(PAIRS):
-        grad = nn(w_ref[PAIR_ROWS * pair : PAIR_ROWS * (pair + 1), :], dout_ref[...]).astype(BF16)
+        grad = nn(w_ref[PAIR_ROWS * pair : PAIR_ROWS * (pair + 1), :], dout).astype(BF16)
         g_ref[me, pair, :PAIR_ROWS, :] = grad
         product = grad.astype(F32) * at_ref[slot, PAIR_ROWS * pair : PAIR_ROWS * (pair + 1), :].astype(F32)
         lines = []
@@ -414,8 +414,7 @@
             lines += terms(delta)
         lines.append(jnp.zeros((STAT_ROWS - 12, rows), F32))
         g_ref[me, pair, PAIR_ROWS:, :] = jnp.concatenate(lines, axis=0).astype(BF16)
-        if pair % 2:
-            g_spread(pair // 2)
+    g_spread(0)
 
     def query_pass(pair):
         low = HEADS + 2 * pair
@@ -427,8 +426,8 @@
         dq_ref[PAIR_ROWS * pair : PAIR_ROWS * (pair + 1), :] = merged(value) * score_scale
 
     def key_pass(pair):
-        if pair % 2 == 0:
-            g_finish(pair // 2)
+        if pair in (0, 3):
+            g_finish(pair // 3)
         queries = whole(QUERY, pair)
         grads = jnp.concatenate([g_ref[j, pair] for j in range(members)], axis=1)
         stats = grads[PAIR_ROWS:]
@@ -552,11 +551,12 @@
     tile_lane = lax.broadcasted_iota(jnp.int32, pack_loss.shape, 1)
     pair_own[...] = jnp.where(tile_lane == 0, pack_loss, length.astype(F32))
     copy(pair_own, pair_all, small_send.at[3], small_recv.at[3], (across, me)).start()
+    pl.when(job == 1)(functools.partial(g_spread, 1))
     weight_part()
-    g_relay(0)
+    pl.when(job == 0)(functools.partial(g_spread, 1))
     query_pass(2)
     query_pass(3)
-    g_relay(1)
+    g_relay(0)
     received(pair_all, small_recv.at[3])
     sum_own[...] = pair_own[...] + pair_all[...]
     for shift in range(1, outer):
@@ -565,11 +565,28 @@
     sum_all[step_a] = sum_own[...]
     kvq_finish(QUERY)
     units = [(i, to) for i in range(mine) for to in (0, 1)]
-    quarter = len(units) // PAIRS
-    for pair in range(PAIRS):
-        key_pass(pair)
-        for i, to in units[pair * quarter : (pair + 1) * quarter]:
-            weight_sum(i, to)
+    quarter = len(units) // 4
+    parts = [units[quarter * k : quarter * (k + 1)] for k in range(4)]
+
+    def weight_sums(early, late):
+        for which, chosen in ((0, early), (1, late)):
+            if chosen:
+
+                @pl.when(job == which)
+                def _():
+                    for i, to in chosen:
+                        weight_sum(i, to)
+
+    weight_sums(parts[0] + parts[1], [])
+    key_pass(0)
+    weight_sums(parts[2], [])
+    pl.when(job == 1)(functools.partial(g_relay, 1))
+    key_pass(1)
+    weight_sums(parts[3], parts[0])
+    pl.when(job == 0)(functools.partial(g_relay, 1))
+    key_pass(2)
+    weight_sums([], parts[1] + parts[2] + parts[3])
+    key_pass(3)
 
     received(sum_all.at[pl.ds(0, outer - 1)], small_recv.at[2])
     totals = sum_all[0]
@@ -657,7 +674,6 @@
                 pltpu.VMEM((rows, WIDTH), BF16),
                 pltpu.VMEM((PAIRS, groups, share, PAIR_ROWS), BF16),
                 pltpu.VMEM((WIDTH, rows), F32),
-                pltpu.VMEM((WIDTH, rows), BF16),
                 pltpu.VMEM((3, members, FEAT, rows), BF16),
                 pltpu.VMEM((members, PAIRS, AUG_ROWS, rows), BF16),
                 pltpu.VMEM((1, rows), jnp.int32),

time: 29.6 us -> 29.3 us (0.990)
  the two profiles are of different devices: /device:TPU:0 before, /device:TPU:1 now
where the time goes in v6:
time: 29.3 us; the launch traced here: 29.2 us
  Pallas kernels  27.9 us (95%)
  between operations  1.29 us (4%)
    pallas_call x1, Pallas kernels, local(): pl.pallas_call(functools.partial(kernel, members, groups), out_shape=(jax...  26.8 us
    pallas_call x1, Pallas kernels, local(): pl.pallas_call(functools.partial(scale_kernel, groups * total, total), ou...  1.09 us

profile of v6, /device:TPU:1, one launch (start us, length us, event | category | flops | bytes accessed | tf_op | source)
XLA Modules:
  0.0 29.2 jit_solution(10193743068586167325)
XLA Ops:
  1.3 26.8 %sublayer.1 = (f32[576,128]{1,0:T(8,128)S(1)}, f32[576,128]{1,0:T(8,128)S(1)}, f32[576,128]{1,0:T(8,128)S(1)}, f32[144,144]{1,0:T(8,128)S(1)}, f32[8,128]{1,0:T(8,128)S(1)}) custom-call(s32[1]{0:T(128)S(6)} %copy.12.len_ref, s32[1,128]{1,0:T(1,128)} %seg_hbm.1, bf16[576,128]{1,0:T(8,128)(2,1)} %bitcast.21, bf16[576,128]{1,0:T(8,128)(2,1)} %bitcast.22, ...), custom_call_target="tpu_custom_call" | custom-call | tf_op jit(solution)/shard_map/sublayer/pallas_call | solution.py:661
  28.1 1.1 %scale.1 = (f32[576,128]{1,0:T(8,128)}, f32[576,128]{1,0:T(8,128)}, f32[576,128]{1,0:T(8,128)}, f32[144,144]{1,0:T(8,128)}, f32[1,1]{1,0:T(1,128)}) custom-call(f32[8,128]{1,0:T(8,128)S(1)} %get-tuple-element.15.sum_ref, f32[576,128]{1,0:T(8,128)S(1)} %get-tuple-element.16.dq_ref, f32[576,128]{1,0:T(8,128)S(1)} %get-tuple-element.17.dk_ref, ...), custom_call_target="tpu_custom_call" | custom-call | tf_op jit(solution)/shard_map/scale/pallas_call | solution.py:720

commit v7 on v6

--- a/solution.py
+++ b/solution.py
@@ -84,6 +84,9 @@
     y_all,
     z_own,
     z_all,
+    zb_all,
+    yb_own,
+    yb_all,
     tile_own,
     tile_all,
     pair_own,
@@ -108,6 +111,8 @@
     small_send,
     small_recv,
     wave_sem,
+    turn_send,
+    turn_recv,
 ):
     rows = q_hbm.shape[1]
     chips = members // 2
@@ -123,6 +128,9 @@
     across = step_a * 2 + 1 - step_b
     slot = step_b * 2 + core
     job = (core + chip) % 2
+    detour = chips == 2
+    turn_owner = job * mine
+    ends_turn = step_a % mine == 0
 
     def patch_peer(shift):
         return lax.rem(me + shift, members)
@@ -455,6 +463,17 @@
                 value = value + nn(wt_ref[pair, block], attention(pair))
             other_ref[i] = value
 
+    def deliver(block, everyone, to, send, recv, owner):
+        stays = jnp.logical_and(owner == step_a, core == to)
+
+        @pl.when(stays)
+        def _():
+            everyone[step_a] = block[...]
+
+        @pl.when(jnp.logical_not(stays))
+        def _():
+            copy(block, everyone.at[step_a], send, recv, (owner * 2 + step_b, chip * 2 + to)).start()
+
     def weight_blocks(away, blocks, grads, attn, span):
         if main:
             attn_main = jnp.concatenate([attn[p * features : p * features + main] for p in range(span)], axis=0)
@@ -485,6 +504,9 @@
         def send(i, shift):
             away = far(shift)
             for to in (0, 1):
+                if detour and (i, to) == (0, 1):
+                    deliver(u_own.at[i, away * 2 + to], zb_all, 0, turn_send.at[0], turn_recv.at[0], turn_owner)
+                    continue
                 copy(
                     u_own.at[i, away * 2 + to],
                     y_all.at[i, to, chip],
@@ -506,6 +528,8 @@
                     weight_blocks(far(shift) * 2, [i], grads[i], attn_of(shift), 2)
                     send(i, shift)
             weight_blocks(chip * 2, range(mine), jnp.concatenate(grads, axis=0), attn_of(0), 2)
+            if detour:
+                deliver(u_own.at[0, chip * 2 + 1], z_all, 1, z_send.at[0], z_recv.at[0], turn_owner)
         else:
             attn = jnp.concatenate([at_ref[s] for s in range(4)], axis=1)
             for i in range(mine):
@@ -514,27 +538,44 @@
                     send(i, shift)
 
     def weight_sum(i, to):
+        if detour and (i, to) == (0, 1):
+            return
         received(y_all.at[i, to, pl.ds(0, chips - 1)], y_recv.at[i, to])
         value = u_own[i, chip * 2 + to].astype(F32)
         for shift in range(1, chips):
             value = value + y_all[i, to, far(shift)].astype(F32)
         z_own[i, to] = value.astype(BF16)
-        owner = job * mine + i
-        stays = jnp.logical_and(owner == step_a, core == to)
-
-        @pl.when(stays)
-        def _():
-            z_all[step_a] = z_own[i, to]
-
-        @pl.when(jnp.logical_not(stays))
-        def _():
-            copy(
-                z_own.at[i, to],
-                z_all.at[step_a],
-                z_send.at[0],
-                z_recv.at[0],
-                (owner * 2 + step_b, chip * 2 + to),
-            ).start()
+        deliver(z_own.at[i, to], z_all, to, z_send.at[0], z_recv.at[0], job * mine + i)
+
+    def turn():
+        @pl.when(jnp.logical_and(ends_turn, core == 0))
+        def _():
+            @pl.when(job == step_a // mine)
+            def _():
+                received(zb_all.at[pl.ds(0, outer - 1)], turn_recv.at[0])
+
+            @pl.when(job != step_a // mine)
+            def _():
+                received(zb_all, turn_recv.at[0])
+
+            value = zb_all[0].astype(F32)
+            for j in range(1, outer):
+                value = value + zb_all[j].astype(F32)
+            yb_own[...] = value.astype(BF16)
+            copy(yb_own, yb_all, turn_send.at[1], turn_recv.at[1], (dp, far(1) * 2 + 1)).start()
+
+    def turn_end():
+        @pl.when(jnp.logical_not(jnp.logical_and(turn_owner == step_a, core == 0)))
+        def _():
+            sent(yb_own, turn_send.at[0])
+
+        @pl.when(jnp.logical_and(ends_turn, core == 0))
+        def _():
+            sent(yb_own, turn_send.at[1])
+
+        @pl.when(jnp.logical_and(ends_turn, core == 1))
+        def _():
+            received(yb_all, turn_recv.at[1])
 
     for hops in range(4, outer + 1):
         wave_wait()
@@ -584,6 +625,8 @@
     key_pass(1)
     weight_sums(parts[3], parts[0])
     pl.when(job == 0)(functools.partial(g_relay, 1))
+    if detour:
+        turn()
     key_pass(2)
     weight_sums([], parts[1] + parts[2] + parts[3])
     key_pass(3)
@@ -598,7 +641,11 @@
     sent(g_ref.at[pl.ds(0, members - 1)], g_send.at[0])
     sent(at_ref.at[pl.ds(0, 3)], at_send.at[0])
     sent(tt_all.at[pl.ds(0, 3)], tt_send.at[0])
-    sent(y_all.at[:, :, pl.ds(0, chips - 1)], y_send.at[0])
+    if detour:
+        sent(z_all.at[pl.ds(0, 2 * mine - 1)], y_send.at[0])
+        turn_end()
+    else:
+        sent(y_all.at[:, :, pl.ds(0, chips - 1)], y_send.at[0])
     sent(seg_all.at[pl.ds(0, members - 1)], small_send.at[0])
     sent(tile_all.at[pl.ds(0, members - 1)], small_send.at[1])
     sent(sum_all.at[pl.ds(0, outer - 1)], small_send.at[2])
@@ -619,6 +666,8 @@
     summed = z_all[0].astype(F32)
     for j in range(1, outer):
         summed = summed + z_all[j].astype(F32)
+    if detour:
+        summed = summed + jnp.where(jnp.logical_and(ends_turn, core == 1), yb_all[...].astype(F32), 0.0)
     if main:
         dw_ref[:main, :] = summed[:share].T
     for t in range(tiles):
@@ -689,6 +738,9 @@
                 pltpu.VMEM((mine, 2, chips, unit_rows, LANES), BF16),
                 pltpu.VMEM((mine, 2, unit_rows, LANES), BF16),
                 pltpu.VMEM((outer, unit_rows, LANES), BF16),
+                pltpu.VMEM((outer, unit_rows, LANES), BF16),
+                pltpu.VMEM((unit_rows, LANES), BF16),
+                pltpu.VMEM((unit_rows, LANES), BF16),
                 pltpu.VMEM((8, 128), F32),
                 pltpu.VMEM((members, 8, 128), F32),
                 pltpu.VMEM((8, 128), F32),
@@ -713,6 +765,8 @@
                 dma((4,)),
                 dma((4,)),
                 pltpu.SemaphoreType.REGULAR((2,)),
+                dma((2,)),
+                dma((2,)),
             ],
             compiler_params=pltpu.CompilerParams(collective_id=0, has_side_effects=True, vmem_limit_bytes=48000000),
             name="sublayer",

time: 29.3 us -> 28.9 us (0.986)
  the two profiles are of different devices: /device:TPU:1 before, /device:TPU:0 now
where the time goes in v7:
time: 28.9 us; the launch traced here: 28.7 us
  Pallas kernels  27.4 us (95%)
  between operations  1.29 us (4%)
    pallas_call x1, Pallas kernels, local(): pl.pallas_call(functools.partial(kernel, members, groups), out_shape=(jax...  26.3 us
    pallas_call x1, Pallas kernels, local(): pl.pallas_call(functools.partial(scale_kernel, groups * total, total), ou...  1.09 us

profile of v7, /device:TPU:0, one launch (start us, length us, event | category | flops | bytes accessed | tf_op | source)
XLA Modules:
  0.0 28.7 jit_solution(12097565655044690091)
XLA Ops:
  1.3 26.3 %sublayer.1 = (f32[576,128]{1,0:T(8,128)S(1)}, f32[576,128]{1,0:T(8,128)S(1)}, f32[576,128]{1,0:T(8,128)S(1)}, f32[144,144]{1,0:T(8,128)S(1)}, f32[8,128]{1,0:T(8,128)S(1)}) custom-call(s32[1]{0:T(128)S(6)} %copy.12.len_ref, s32[1,128]{1,0:T(1,128)} %seg_hbm.1, bf16[576,128]{1,0:T(8,128)(2,1)} %bitcast.21, bf16[576,128]{1,0:T(8,128)(2,1)} %bitcast.22, ...), custom_call_target="tpu_custom_call" | custom-call | tf_op jit(solution)/shard_map/sublayer/pallas_call | solution.py:710
  27.6 1.1 %scale.1 = (f32[576,128]{1,0:T(8,128)}, f32[576,128]{1,0:T(8,128)}, f32[576,128]{1,0:T(8,128)}, f32[144,144]{1,0:T(8,128)}, f32[1,1]{1,0:T(1,128)}) custom-call(f32[8,128]{1,0:T(8,128)S(1)} %get-tuple-element.15.sum_ref, f32[576,128]{1,0:T(8,128)S(1)} %get-tuple-element.16.dq_ref, f32[576,128]{1,0:T(8,128)S(1)} %get-tuple-element.17.dk_ref, ...), custom_call_target="tpu_custom_call" | custom-call | tf_op jit(solution)/shard_map/scale/pallas_call | solution.py:774
